TPU v7x, 32 devices: a whole 2x2x4 slice. The times are simulated.
32 devices in a mesh: sx: 4 (over y, x), sy: 8 (over z, core).
Axes of the slice: x: 2, y: 2, z: 4, core: 2. Of those that a mesh axis runs over, the one named last changes fastest.
Arguments:
- forward_weights: float32 [4096, 8, 432], P(('sy', 'sx')), may hold values from -6 to 6
- adjoint_weights: float32 [32768, 432], P(('sx', 'sy')), may hold values from -6 to 6
- medium: float32 [4], replicated, may hold values from 0.2 to 0.6
Outputs:
- forward_out: float32 [32768, 432], P(('sx', 'sy'))
- adjoint_out: float32 [8, 4096, 432], P(None, ('sy', 'sx'))
All inputs are finite; a program needn't handle non-finite values.
Results may differ from a plain program's by a relative error of at most 0.0003.
Values sent between devices are 32-bit elements; how exact they have to be, the bound alone decides.
A program may use at most 128 MiB of HBM per device.

v0:
```python
import math

import jax
import jax.numpy as jnp
import ml_dtypes
import numpy as np
from jax import lax
from jax.experimental import pallas as pl
from jax.experimental.pallas import tpu as pltpu
from jax.sharding import PartitionSpec as P

ORDER = 6
LEVELS = 4
Q = 216
band = 8.0


def cheb_points(n):
    return np.array([(1.0 - math.cos((2 * i + 1) * math.pi / (2 * n))) / 2.0 for i in range(n)])


def child_table(n):
    g = cheb_points(n)
    halves = []
    for bit in range(2):
        m = np.ones((n, n))
        for r in range(n):
            w = (g[r] + bit) / 2.0
            for c in range(n):
                for o in range(n):
                    if o != c:
                        m[r, c] *= (w - g[o]) / (g[c] - g[o])
        halves.append(m)
    return np.stack(
        [np.kron(np.kron(halves[e // 4], halves[e // 2 % 2]), halves[e % 2]) for e in range(8)]
    )


def split_table(table):
    high = table.astype(ml_dtypes.bfloat16)
    low = (table - high.astype(np.float64)).astype(ml_dtypes.bfloat16)
    return jnp.asarray(high), jnp.asarray(low)


def box_coords(index, groups):
    coords = [jnp.zeros_like(index) for _ in range(3)]
    for group in range(groups):
        digit = index // 8 ** (groups - 1 - group) % 8
        bits = (digit // 4, digit // 2 % 2, digit % 2)
        coords = [c * 2 + b for c, b in zip(coords, bits)]
    return [c.astype(jnp.float32) for c in coords]


def point_slopes(src_off, count, groups, medium):
    side = band / float(2**groups)
    g = cheb_points(ORDER).astype(np.float32)
    grid = (np.repeat(g, ORDER * ORDER), np.tile(np.repeat(g, ORDER), ORDER), np.tile(g, ORDER**2))
    corner = box_coords(src_off + jnp.arange(count, dtype=jnp.int32), groups)
    pts = [side * (c[:, None] + o[None, :]) for c, o in zip(corner, grid)]
    radius = jnp.sqrt(pts[0] * pts[0] + pts[1] * pts[1] + pts[2] * pts[2])
    return [p + medium[d + 1] * radius for d, p in enumerate(pts)], medium[0] * radius


def turn_of(u):
    half = jnp.round(2.0 * u)
    y = (2.0 * math.pi) * (u - 0.5 * half)
    sign = 1.0 - 2.0 * (half - 2.0 * jnp.floor(0.5 * half))
    z = y * y
    s = jnp.float32(-1.0 / math.factorial(11))
    for n in (9, 7, 5, 3, 1):
        s = s * z + (1.0 if n % 4 == 1 else -1.0) / math.factorial(n)
    c = jnp.float32(1.0 / math.factorial(12))
    for n in (10, 8, 6, 4, 2, 0):
        c = c * z + (1.0 if n % 4 == 0 else -1.0) / math.factorial(n)
    return sign * c, sign * (s * y)


def pair_phase(src_off, src_count, src_groups, tgt_off, tgt_count, tgt_groups, medium):
    slopes, base = point_slopes(src_off, src_count, src_groups, medium)
    coords = box_coords(tgt_off + jnp.arange(tgt_count, dtype=jnp.int32), tgt_groups)
    u = base[:, None, :]
    for c, a in zip(coords, slopes):
        u = u + ((c + 0.5) / float(2**tgt_groups))[None, :, None] * a[:, None, :]
    return turn_of(u)


def child_phase(src_off, src_count, level, medium):
    slopes, _ = point_slopes(src_off, src_count, LEVELS - level, medium)
    k = np.arange(8)
    u = 0.0
    for bits, a in zip((k // 4, k // 2 % 2, k % 2), slopes):
        step = ((bits - 0.5) / 2.0 ** (level + 2)).astype(np.float32)
        u = u + step[None, :, None] * a[:, None, :]
    return jnp.stack(turn_of(u), axis=1)


def dot3(x, high, low):
    x_high = x.astype(jnp.bfloat16)
    x_low = (x - x_high.astype(jnp.float32)).astype(jnp.bfloat16)
    dot = lambda a, b: jnp.dot(a, b, preferred_element_type=jnp.float32)
    return dot(x_high, high) + dot(x_high, low) + dot(x_low, high)


def forward_kernel(x_ref, w_ref, high_ref, low_ref, o_ref):
    pb, _, _, tb, q = o_ref.shape[0], 2, 8, o_ref.shape[3], o_ref.shape[4]

    def step(e, acc):
        parts = []
        for p in range(pb):
            re, im = x_ref[p, e, 0], x_ref[p, e, 1]
            w_re, w_im = w_ref[p, e, 0], w_ref[p, e, 1]
            res = [re * w_re[k : k + 1] - im * w_im[k : k + 1] for k in range(8)]
            ims = [re * w_im[k : k + 1] + im * w_re[k : k + 1] for k in range(8)]
            parts += res + ims
        return acc + dot3(jnp.concatenate(parts, axis=0), high_ref[e], low_ref[e])

    acc = lax.fori_loop(0, 8, step, jnp.zeros((pb * 16 * tb, q), jnp.float32))
    o_ref[...] = acc.reshape(o_ref.shape)


def adjoint_kernel(y_ref, w_ref, high_ref, low_ref, o_ref):
    sb, tb, q = y_ref.shape[0], y_ref.shape[3], y_ref.shape[4]
    rows = y_ref[...].reshape(sb * 16 * tb, q)

    def step(e, carry):
        z = dot3(rows, high_ref[e], low_ref[e]).reshape(sb, 2, 8, tb, q)
        for s in range(sb):
            w_re, w_im = w_ref[s, e, 0], w_ref[s, e, 1]
            out_re = jnp.zeros((tb, q), jnp.float32)
            out_im = jnp.zeros((tb, q), jnp.float32)
            for k in range(8):
                re, im = z[s, 0, k], z[s, 1, k]
                c, d = w_re[k : k + 1], w_im[k : k + 1]
                out_re += re * c + im * d
                out_im += im * c - re * d
            o_ref[s, e, 0] = out_re
            o_ref[s, e, 1] = out_im
        return carry

    lax.fori_loop(0, 8, step, 0)


def blocks(count, tgt):
    tb = min(tgt, 32)
    return math.gcd(count, max(1, 32 // tb)), tb


def level_call(kernel, operand, phase, tables, out_shape):
    count, tgt, q = operand.shape[0], operand.shape[3], operand.shape[4]
    cb, tb = blocks(count, tgt)
    spec = lambda: pl.BlockSpec((cb, operand.shape[1], operand.shape[2], tb, q), lambda i, j: (i, 0, 0, j, 0))
    return pl.pallas_call(
        kernel,
        grid=(count // cb, tgt // tb),
        in_specs=[
            spec(),
            pl.BlockSpec((cb,) + phase.shape[1:], lambda i, j: (i, 0, 0, 0, 0)),
            pl.BlockSpec(tables[0].shape, lambda i, j: (0, 0, 0)),
            pl.BlockSpec(tables[1].shape, lambda i, j: (0, 0, 0)),
        ],
        out_specs=pl.BlockSpec((cb, out_shape[1], out_shape[2], tb, q), lambda i, j: (i, 0, 0, j, 0)),
        out_shape=jax.ShapeDtypeStruct(out_shape, jnp.float32),
        compiler_params=pltpu.CompilerParams(vmem_limit_bytes=56 * 1024 * 1024),
    )(operand, phase, *tables)


def forward_level(x, src_off, level, medium, tables):
    count, _, tgt, q = x.shape
    phase = child_phase(src_off, count, level, medium).reshape(count // 8, 8, 2, 8, q)
    out = level_call(
        forward_kernel, x.reshape(count // 8, 8, 2, tgt, q), phase, tables, (count // 8, 2, 8, tgt, q)
    )
    return out.swapaxes(2, 3).reshape(count // 8, 2, tgt * 8, q)


def adjoint_level(y, src_off, level, medium, tables):
    count, _, tgt, q = y.shape
    phase = child_phase(src_off * 8, count * 8, level, medium).reshape(count, 8, 2, 8, q)
    operand = y.reshape(count, 2, tgt // 8, 8, q).swapaxes(2, 3)
    out = level_call(adjoint_kernel, operand, phase, tables, (count, 8, 2, tgt // 8, q))
    return out.reshape(count * 8, 2, tgt // 8, q)


def shards(forward_weights, adjoint_weights, medium):
    table = child_table(ORDER) / math.sqrt(8.0)
    forward_tables = split_table(table)
    adjoint_tables = split_table(table.transpose(0, 2, 1))
    sizes = {a: lax.axis_size(a) for a in ("sx", "sy")}
    index = {a: lax.axis_index(a) for a in ("sx", "sy")}
    local_sources = forward_weights.shape[0]
    shots = forward_weights.shape[2] // (2 * Q)
    plan = []
    remaining = ["sx", "sy"]
    width = local_sources
    for _ in range(LEVELS):
        while width < 8:
            axis = remaining.pop(0)
            plan.append(axis)
            width *= sizes[axis]
        plan.append("level")
        width //= 8

    f_in = forward_weights.reshape(local_sources, -1, 2, shots, Q)
    b_in = adjoint_weights.reshape(adjoint_weights.shape[0], 2, shots, Q)
    f_src = (index["sy"] * sizes["sx"] + index["sx"]) * local_sources
    b_tgt = (index["sx"] * sizes["sy"] + index["sy"]) * adjoint_weights.shape[0]
    f_outs, b_outs = [], []
    for shot in range(shots):
        src, tgt, level = f_src, jnp.int32(0), 0
        re, im = f_in[:, :, 0, shot], f_in[:, :, 1, shot]
        c, s = pair_phase(src, re.shape[0], LEVELS, tgt, re.shape[1], 1, medium)
        x = jnp.stack([re * c - im * s, re * s + im * c], axis=1)
        for op in plan:
            if op == "level":
                x = forward_level(x, src, level, medium, forward_tables)
                src, tgt, level = src // 8, tgt * 8, level + 1
            else:
                n = sizes[op]
                count, _, width, _ = x.shape
                x = x.reshape(count, 2, n, width // n, Q).transpose(2, 0, 1, 3, 4)
                x = lax.all_to_all(x, op, split_axis=0, concat_axis=0, tiled=True)
                x = x.reshape(n * count, 2, width // n, Q)
                src = src - index[op] * count
                tgt = tgt + index[op] * (width // n)
        c, s = pair_phase(src, x.shape[0], LEVELS - level, tgt, x.shape[2], level + 1, medium)
        re, im = x[:, 0], x[:, 1]
        f_outs.append((re * c + im * s, im * c - re * s))
        src, tgt, level = jnp.int32(0), b_tgt, LEVELS
        re, im = b_in[None, :, 0, shot], b_in[None, :, 1, shot]
        c, s = pair_phase(src, 1, 0, tgt, re.shape[1], LEVELS + 1, medium)
        y = jnp.stack([re * c - im * s, re * s + im * c], axis=1)
        for op in reversed(plan):
            if op == "level":
                y = adjoint_level(y, src, level - 1, medium, adjoint_tables)
                src, tgt, level = src * 8, tgt // 8, level - 1
            else:
                n = sizes[op]
                count, _, width, _ = y.shape
                y = y.reshape(n, count // n, 2, width, Q)
                y = lax.all_to_all(y, op, split_axis=0, concat_axis=0, tiled=True)
                y = y.transpose(1, 2, 0, 3, 4).reshape(count // n, 2, n * width, Q)
                src = src + index[op] * (count // n)
                tgt = tgt - index[op] * width
        c, s = pair_phase(src, y.shape[0], LEVELS, tgt, y.shape[2], 1, medium)
        re, im = y[:, 0], y[:, 1]
        b_outs.append((re * c + im * s, im * c - re * s))
    f = jnp.stack([jnp.stack([o[i][0] for o in f_outs], axis=1) for i in range(2)], axis=1)
    b = jnp.stack([jnp.stack([o[i].swapaxes(0, 1) for o in b_outs], axis=2) for i in range(2)], axis=2)
    return f.reshape(f.shape[0], -1), b.reshape(b.shape[0], b.shape[1], -1)


def solution(mesh):
    in_specs = (P(("sy", "sx"), None, None), P(("sx", "sy"), None), P())
    out_specs = (P(("sx", "sy"), None), P(None, ("sy", "sx"), None))
    return jax.shard_map(shards, mesh=mesh, in_specs=in_specs, out_specs=out_specs, check_vma=False)
```

profile of v0, /device:TPU:0, one launch (start us, length us, event | category | flops | bytes accessed | tf_op | source)
XLA Modules:
  0.0 274.4 jit_solution(4529691224481224079)
XLA Ops:
  1.1 1.5 fusion.439
  2.6 1.6 fusion.438
  4.2 0.5 copy.175
  4.7 0.5 copy.174
  5.2 2.8 %multiply_add_fusion.14 = (f32[16,8,216]{2,1,0:T(8,128)S(1)}, f32[16,8,216]{2,1,0:T(8,128)S(1)}, f32[16,8,216]{2,1,0:T(8,128)S(1)}, f32[16,8,216]{2,1,0:T(8,128)...) fusion(f32[16,8]{1,0:T(8,128)S(1)} %get-tuple-element.104, ...), kind=kLoop, calls=%fused_computation.175 | loop fusion | flops 967680 | bytes 779824 | tf_op jit(solution)/shard_map/add | solution.py:61
  8.0 5.5 %fusion.16 = (f32[16,8,1,8,216]{4,3,2,1,0:T(8,128)}, f32[16,8,1,8,216]{4,3,2,1,0:T(8,128)}, f32[16,8,1,8,216]{4,3,2,1,0:T(8,128)S(1)}, f32[16,8,1,8,216]{4,3,2,1...) fusion(f32[16,8,216]{2,1,0:T(8,128)S(1)} %get-tuple-element.25, ...), kind=kLoop, calls=%fused_computation.54 | loop fusion | flops 28753920 | bytes 7852224 | tf_op jit(solution)/shard_map/mul | solution.py:75
  13.5 1.5 pad_maximum_fusion.x_ref
  15.1 1.5 pad_maximum_fusion.1.w_ref
  16.6 16.0 %shard_map.626 = f32[16,2,8,8,216]{4,3,2,1,0:T(8,128)} custom-call(f32[16,8,2,8,216]{4,3,2,1,0:T(8,128)} %pad_maximum_fusion.x_ref, f32[16,8,2,8,216]{4,3,2,1,0:T(8,128)} %pad_maximum_fusion.1.w_ref, bf16[8,216,216]{2,1,0:T(8,128)(2,1)} %constant.1564.clone.high_ref, bf16[8,216,216]{2,1,0:T(8,128)(2,1)} %constant.1565.clone.low_ref), custom_call_target="tpu_custom_call" | custom-call | tf_op jit(solution)/shard_map/pallas_call | solution.py:152
  32.6 3.9 %copy.147 = f32[16,2,8,8,216]{4,3,2,1,0:T(8,128)} copy(f32[16,2,8,8,216]{4,2,3,1,0:T(8,128)} %bitcast.112) | data formatting | bytes 3538944 | tf_op jit(solution)/shard_map/transpose | solution.py:173
  36.4 1.9 add_add_fusion.2
  38.4 1.1 fusion.66
  39.5 0.7 pad_maximum_fusion.5.w_ref
  40.2 16.0 %shard_map.627 = f32[2,2,8,64,216]{4,3,2,1,0:T(8,128)} custom-call(f32[2,8,2,64,216]{4,3,2,1,0:T(8,128)} %bitcast.94, f32[2,8,2,8,216]{4,3,2,1,0:T(8,128)} %pad_maximum_fusion.5.w_ref, bf16[8,216,216]{2,1,0:T(8,128)(2,1)} %constant.1564.clone.high_ref, bf16[8,216,216]{2,1,0:T(8,128)(2,1)} %constant.1565.clone.low_ref), custom_call_target="tpu_custom_call" | custom-call | tf_op jit(solution)/shard_map/pallas_call | solution.py:152
  56.2 2.8 %copy.148 = f32[2,2,64,8,216]{4,3,2,1,0:T(8,128)S(1)} copy(f32[2,2,64,8,216]{4,2,3,1,0:T(8,128)} %bitcast.96) | data formatting | bytes 3538944 | tf_op jit(solution)/shard_map/transpose | solution.py:173
  59.0 1.7 copy.149
  60.8 5.3 %all-to-all-start = ((f32[4,2,2,128,216]{3,4,2,1,0:T(8,128)}), f32[4,2,2,128,216]{3,4,2,1,0:T(8,128)S(1)}, u32[]{:S(2)}, u32[]{:S(2)}) async-start(f32[4,2,2,128,216]{3,4,2,1,0:T(8,128)} %copy.149), calls=%async_computation | async-start | bytes 3538944 | tf_op jit(solution)/shard_map/all_to_all | solution.py:221
  66.1 0.6 add_convert_fusion.3
  66.8 0.6 fusion.430
  67.3 0.6 fusion.398
  67.9 0.6 fusion.433
  68.5 0.6 fusion.394
  69.1 0.6 add_convert_fusion.4
  69.7 1.3 fusion.437
  71.2 1.5 copy.177
  72.7 2.5 copy.176
  75.4 1.9 multiply_add_fusion.26
  77.6 0.7 maximum_bitcast_fusion.3.w_ref
  78.3 2.5 broadcast_multiply_fusion
  80.8 3.1 %multiply_subtract_fusion.2 = (f32[1,1,128,8,216]{4,2,3,1,0:T(8,128)S(1)}, f32[1,1,128,8,216]{4,2,3,1,0:T(8,128)S(1)}) fusion(f32[1,1,128,8,216]{4,3,2,1,0:T(8,128)S(1)} %bitcast.113, f32[1,1,128,8,216]{4,3,2,1,0:T(8,128)} %bitcast.114, f32[216]{0:T(256)S(1)} %bitcast.123, f32[128,8]{0,1:T(8,128)S(1)} %fusion.321, f32[216]{0:T(256)S(1)} %bitcast.125, ...), kind=kLoop, calls=%fused_computation.63 | loop fusion | flops 10616832 | bytes 3554688 | tf_op jit(solution)/shard_map/sub | solution.py:231
  83.9 1.5 maximum_bitcast_fusion.y_ref
  85.4 14.8 %shard_map.630 = f32[1,8,2,128,216]{4,3,2,1,0:T(8,128)} custom-call(f32[1,2,8,128,216]{4,3,2,1,0:T(8,128)} %maximum_bitcast_fusion.y_ref, f32[1,8,2,8,216]{4,3,2,1,0:T(8,128)} %maximum_bitcast_fusion.3.w_ref, bf16[8,216,216]{2,1,0:T(8,128)(2,1)} %constant.1566.clone.high_ref, bf16[8,216,216]{2,1,0:T(8,128)(2,1)} %constant.1567.clone.low_ref), custom_call_target="tpu_custom_call" | custom-call | tf_op jit(solution)/shard_map/pallas_call | solution.py:152
  100.2 2.8 %copy.165 = f32[8,1,2,128,216]{3,4,2,1,0:T(8,128)} copy(f32[8,1,2,128,216]{4,3,2,0,1:T(8,128)} %bitcast.102) | data formatting | bytes 3538944 | tf_op jit(solution)/shard_map/reshape;reshape | solution.py:239
  103.0 5.0 %all-to-all-start.2 = ((f32[8,1,2,128,216]{3,4,2,1,0:T(8,128)}), f32[8,1,2,128,216]{3,4,2,1,0:T(8,128)}, u32[]{:S(2)}, u32[]{:S(2)}) async-start(f32[8,1,2,128,216]{3,4,2,1,0:T(8,128)} %copy.165), calls=%async_computation.2 | async-start | bytes 3538944 | tf_op jit(solution)/shard_map/all_to_all | solution.py:240
  108.3 0.7 maximum_bitcast_fusion.1.w_ref
  109.0 1.9 copy.150
  110.8 16.0 %shard_map.628 = f32[1,2,8,128,216]{4,3,2,1,0:T(8,128)} custom-call(f32[1,8,2,128,216]{4,3,2,1,0:T(8,128)} %bitcast.103, f32[1,8,2,8,216]{4,3,2,1,0:T(8,128)} %maximum_bitcast_fusion.1.w_ref, bf16[8,216,216]{2,1,0:T(8,128)(2,1)} %constant.1564.clone.high_ref, bf16[8,216,216]{2,1,0:T(8,128)(2,1)} %constant.1565.clone.low_ref), custom_call_target="tpu_custom_call" | custom-call | tf_op jit(solution)/shard_map/pallas_call | solution.py:152
  126.8 2.8 %copy.151 = f32[1,2,128,8,216]{4,3,2,1,0:T(8,128)S(1)} copy(f32[1,2,128,8,216]{4,2,3,1,0:T(8,128)} %bitcast.97) | data formatting | bytes 3538944 | tf_op jit(solution)/shard_map/transpose | solution.py:173
  129.6 1.7 copy.152
  131.4 18.8 %all-to-all-done.2 = f32[8,1,2,128,216]{3,4,2,1,0:T(8,128)} async-done(((f32[8,1,2,128,216]{3,4,2,1,0:T(8,128)}), f32[8,1,2,128,216]{3,4,2,1,0:T(8,128)}, u32[]{:S(2)}, u32[]{:S(2)}) %all-to-all-start.2) | async-done | bytes 1769504 | tf_op jit(solution)/shard_map/all_to_all | solution.py:240
  150.1 4.3 %all-to-all-start.1 = ((f32[8,1,2,128,216]{3,4,2,1,0:T(8,128)}), f32[8,1,2,128,216]{3,4,2,1,0:T(8,128)}, u32[]{:S(2)}, u32[]{:S(2)}) async-start(f32[8,1,2,128,216]{3,4,2,1,0:T(8,128)} %copy.152), calls=%async_computation.1 | async-start | bytes 3538944 | tf_op jit(solution)/shard_map/all_to_all | solution.py:221
  154.8 0.7 maximum_bitcast_fusion.4.w_ref
  155.4 1.9 copy.166
  157.3 1.9 copy.189
  159.3 14.8 %shard_map.631 = f32[1,8,2,128,216]{4,3,2,1,0:T(8,128)} custom-call(f32[1,2,8,128,216]{4,3,2,1,0:T(8,128)} %bitcast.98, f32[1,8,2,8,216]{4,3,2,1,0:T(8,128)} %maximum_bitcast_fusion.4.w_ref, bf16[8,216,216]{2,1,0:T(8,128)(2,1)} %constant.1566.clone.high_ref, bf16[8,216,216]{2,1,0:T(8,128)(2,1)} %constant.1567.clone.low_ref), custom_call_target="tpu_custom_call" | custom-call | tf_op jit(solution)/shard_map/pallas_call | solution.py:152
  174.1 2.8 %copy.168 = f32[4,2,2,128,216]{3,4,2,1,0:T(8,128)} copy(f32[4,2,2,128,216]{4,3,2,1,0:T(8,128)} %bitcast.104) | data formatting | bytes 3538944 | tf_op jit(solution)/shard_map/reshape;reshape | solution.py:239
  176.9 19.5 %all-to-all-done.1 = f32[8,1,2,128,216]{3,4,2,1,0:T(8,128)} async-done(((f32[8,1,2,128,216]{3,4,2,1,0:T(8,128)}), f32[8,1,2,128,216]{3,4,2,1,0:T(8,128)}, u32[]{:S(2)}, u32[]{:S(2)}) %all-to-all-start.1) | async-done | bytes 1769504 | tf_op jit(solution)/shard_map/all_to_all | solution.py:221
  196.5 4.4 %all-to-all-start.3 = ((f32[4,2,2,128,216]{3,4,2,1,0:T(8,128)}), f32[4,2,2,128,216]{3,4,2,1,0:T(8,128)}, u32[]{:S(2)}, u32[]{:S(2)}) async-start(f32[4,2,2,128,216]{3,4,2,1,0:T(8,128)} %copy.168), calls=%async_computation.3 | async-start | bytes 3538944 | tf_op jit(solution)/shard_map/all_to_all | solution.py:240
  200.9 0.7 maximum_bitcast_fusion.2.w_ref
  201.6 0.7 pad_maximum_fusion.6.w_ref
  202.3 1.5 pad_maximum_fusion.3.w_ref
  203.8 2.6 fusion.80
  206.5 2.9 %copy.153 = f32[8,1,2,128,216]{4,3,2,0,1:T(8,128)} copy(f32[8,1,2,128,216]{3,4,2,1,0:T(8,128)} %all-to-all-done.1) | data formatting | bytes 3538944 | tf_op jit(solution)/shard_map/all_to_all | solution.py:221
  209.3 16.0 %shard_map.629 = f32[1,2,8,128,216]{4,3,2,1,0:T(8,128)} custom-call(f32[1,8,2,128,216]{4,3,2,1,0:T(8,128)} %bitcast.101, f32[1,8,2,8,216]{4,3,2,1,0:T(8,128)} %maximum_bitcast_fusion.2.w_ref, bf16[8,216,216]{2,1,0:T(8,128)(2,1)} %constant.1564.clone.high_ref, bf16[8,216,216]{2,1,0:T(8,128)(2,1)} %constant.1565.clone.low_ref), custom_call_target="tpu_custom_call" | custom-call | tf_op jit(solution)/shard_map/pallas_call | solution.py:152
  225.3 2.8 %copy.190 = f32[1,2,128,8,216]{4,3,2,1,0:T(8,128)S(1)} copy(f32[1,2,128,8,216]{4,2,3,1,0:T(8,128)} %bitcast.95) | data formatting | bytes 3538944 | tf_op jit(solution)/shard_map/transpose | solution.py:173
  228.2 1.9 multiply_add_fusion.4
  230.2 1.7 copy.155
  231.9 1.9 copy.169
  233.8 2.0 copy.188
  235.8 14.9 %shard_map.632 = f32[2,8,2,64,216]{4,3,2,1,0:T(8,128)} custom-call(f32[2,2,8,64,216]{4,3,2,1,0:T(8,128)} %bitcast.99, f32[2,8,2,8,216]{4,3,2,1,0:T(8,128)} %pad_maximum_fusion.6.w_ref, bf16[8,216,216]{2,1,0:T(8,128)(2,1)} %constant.1566.clone.high_ref, bf16[8,216,216]{2,1,0:T(8,128)(2,1)} %constant.1567.clone.low_ref), custom_call_target="tpu_custom_call" | custom-call | tf_op jit(solution)/shard_map/pallas_call | solution.py:152
  250.7 3.8 %copy.187 = f32[16,2,8,8,216]{4,2,3,1,0:T(8,128)} copy(f32[16,2,8,8,216]{4,3,2,1,0:T(8,128)} %bitcast.100) | data formatting | bytes 3538944 | tf_op jit(solution)/shard_map/reshape;reshape | solution.py:179
  254.5 14.9 %shard_map.633 = f32[16,8,2,8,216]{4,3,2,1,0:T(8,128)} custom-call(f32[16,2,8,8,216]{4,3,2,1,0:T(8,128)} %bitcast.111, f32[16,8,2,8,216]{4,3,2,1,0:T(8,128)} %pad_maximum_fusion.3.w_ref, bf16[8,216,216]{2,1,0:T(8,128)(2,1)} %constant.1566.clone.high_ref, bf16[8,216,216]{2,1,0:T(8,128)(2,1)} %constant.1567.clone.low_ref), custom_call_target="tpu_custom_call" | custom-call | tf_op jit(solution)/shard_map/pallas_call | solution.py:152
  269.4 3.0 %add_bitcast_fusion = (f32[8,128,1,1,216]{4,0,1,3,2:T(8,128)S(1)}, f32[8,128,1,1,216]{4,0,1,3,2:T(8,128)S(1)}) fusion(f32[128,2,8,216]{3,2,1,0:T(8,128)} %bitcast.110, f32[128,216]{1,0:T(8,128)S(1)} %get-tuple-element.48, f32[8]{0:T(128)S(1)} %get-tuple-element.128, f32[128,216]{1,0:T(8,128)S(1)} %get-tuple-element.47, f32[8]{0:T(128)S(1)} %get-tuple-element.127, ...), kind=kLoop, calls=%fused_computation.15 | loop fusion | flops 10616832 | bytes 3981408 | tf_op jit(solution)/shard_map/stack;stack | solution.py:248
  272.5 1.8 copy.173
  (92 shorter events, 1.7 us)
Async XLA Ops:
  4.1 1.0 copy-start.5
  4.1 1.0 copy-start.6
  4.2 1.0 copy-start.7
  4.2 3.8 %copy-start.19 = (f32[8]{0:T(128)S(1)}, f32[8]{0:T(128)}, u32[]{:S(2)}) copy-start(f32[8]{0:T(128)} %constant.1588) | copy-start | bytes 100
  4.2 3.8 %copy-start.20 = (f32[8]{0:T(128)S(1)}, f32[8]{0:T(128)}, u32[]{:S(2)}) copy-start(f32[8]{0:T(128)} %constant.1587) | copy-start | bytes 100
  4.2 3.8 %copy-start.21 = (f32[8]{0:T(128)S(1)}, f32[8]{0:T(128)}, u32[]{:S(2)}) copy-start(f32[8]{0:T(128)} %constant.1586) | copy-start | bytes 100
  32.6 5.8 %copy-start.32 = (f32[8]{0:T(128)S(1)}, f32[8]{0:T(128)}, u32[]{:S(2)}) copy-start(f32[8]{0:T(128)} %constant.1591) | copy-start | bytes 100
  32.6 5.8 %copy-start.33 = (f32[8]{0:T(128)S(1)}, f32[8]{0:T(128)}, u32[]{:S(2)}) copy-start(f32[8]{0:T(128)} %constant.1590) | copy-start | bytes 100
  32.6 5.8 %copy-start.34 = (f32[8]{0:T(128)S(1)}, f32[8]{0:T(128)}, u32[]{:S(2)}) copy-start(f32[8]{0:T(128)} %constant.1589) | copy-start | bytes 100
  60.8 8.9 %copy-start.2 = (f32[1024,432]{0,1:T(8,128)S(1)}, f32[1024,432]{0,1:T(8,128)}, u32[]{:S(2)}) copy-start(f32[1024,432]{0,1:T(8,128)} %param.68) | copy-start | bytes 5308420
  60.8 42.2 %all-to-all-start = ((f32[4,2,2,128,216]{3,4,2,1,0:T(8,128)}), f32[4,2,2,128,216]{3,4,2,1,0:T(8,128)S(1)}, u32[]{:S(2)}, u32[]{:S(2)}) async-start(f32[4,2,2,128,216]{3,4,2,1,0:T(8,128)} %copy.149), calls=%async_computation | async-start | bytes 3538944 | tf_op jit(solution)/shard_map/all_to_all | solution.py:221
  71.0 4.2 %copy-start.8 = (f32[8]{0:T(128)S(1)}, f32[8]{0:T(128)}, u32[]{:S(2)}) copy-start(f32[8]{0:T(128)} %get-tuple-element.120) | copy-start | bytes 100
  71.0 4.2 %copy-start.22 = (f32[8]{0:T(128)S(1)}, f32[8]{0:T(128)}, u32[]{:S(2)}) copy-start(f32[8]{0:T(128)} %get-tuple-element.95) | copy-start | bytes 100
  71.0 4.3 %copy-start.23 = (f32[8]{0:T(128)S(1)}, f32[8]{0:T(128)}, u32[]{:S(2)}) copy-start(f32[8]{0:T(128)} %get-tuple-element.96) | copy-start | bytes 100
  71.0 4.3 %copy-start.24 = (f32[8]{0:T(128)S(1)}, f32[8]{0:T(128)}, u32[]{:S(2)}) copy-start(f32[8]{0:T(128)} %get-tuple-element.115) | copy-start | bytes 100
  71.1 4.3 %copy-start.25 = (f32[8]{0:T(128)S(1)}, f32[8]{0:T(128)}, u32[]{:S(2)}) copy-start(f32[8]{0:T(128)} %get-tuple-element.116) | copy-start | bytes 100
  71.1 4.3 %copy-start.26 = (f32[8]{0:T(128)S(1)}, f32[8]{0:T(128)}, u32[]{:S(2)}) copy-start(f32[8]{0:T(128)} %get-tuple-element.121) | copy-start | bytes 100
  71.1 4.3 %copy-start.27 = (f32[8]{0:T(128)S(1)}, f32[8]{0:T(128)}, u32[]{:S(2)}) copy-start(f32[8]{0:T(128)} %get-tuple-element.122) | copy-start | bytes 100
  71.1 4.3 %copy-start.28 = (f32[8]{0:T(128)S(1)}, f32[8]{0:T(128)}, u32[]{:S(2)}) copy-start(f32[8]{0:T(128)} %get-tuple-element.117) | copy-start | bytes 100
  71.1 4.3 %copy-start.29 = (f32[8]{0:T(128)S(1)}, f32[8]{0:T(128)}, u32[]{:S(2)}) copy-start(f32[8]{0:T(128)} %get-tuple-element.118) | copy-start | bytes 100
  71.1 4.3 %copy-start.30 = (f32[8]{0:T(128)S(1)}, f32[8]{0:T(128)}, u32[]{:S(2)}) copy-start(f32[8]{0:T(128)} %get-tuple-element.113) | copy-start | bytes 100
  71.1 4.3 %copy-start.31 = (f32[8]{0:T(128)S(1)}, f32[8]{0:T(128)}, u32[]{:S(2)}) copy-start(f32[8]{0:T(128)} %get-tuple-element.114) | copy-start | bytes 100
  71.1 6.2 %copy-start.16 = (f32[8]{0:T(128)S(1)}, f32[8]{0:T(128)}, u32[]{:S(2)}) copy-start(f32[8]{0:T(128)} %constant.1597) | copy-start | bytes 100
  71.1 6.2 %copy-start.17 = (f32[8]{0:T(128)S(1)}, f32[8]{0:T(128)}, u32[]{:S(2)}) copy-start(f32[8]{0:T(128)} %constant.1596) | copy-start | bytes 100
  71.1 6.2 %copy-start.18 = (f32[8]{0:T(128)S(1)}, f32[8]{0:T(128)}, u32[]{:S(2)}) copy-start(f32[8]{0:T(128)} %constant.1595) | copy-start | bytes 100
  71.2 7.1 %copy-start.9 = (f32[1,216]{1,0:T(1,128)S(1)}, f32[1,216]{1,0:T(1,128)}, u32[]{:S(2)}) copy-start(f32[1,216]{1,0:T(1,128)} %constant.1607) | copy-start | bytes 2596
  71.2 7.1 %copy-start.10 = (f32[1,216]{1,0:T(1,128)S(1)}, f32[1,216]{1,0:T(1,128)}, u32[]{:S(2)}) copy-start(f32[1,216]{1,0:T(1,128)} %constant.1610) | copy-start | bytes 2596
  71.2 7.1 %copy-start.11 = (f32[1,216]{1,0:T(1,128)S(1)}, f32[1,216]{1,0:T(1,128)}, u32[]{:S(2)}) copy-start(f32[1,216]{1,0:T(1,128)} %constant.1609) | copy-start | bytes 2596
  71.2 7.1 %copy-start.12 = (f32[1,216]{1,0:T(1,128)S(1)}, f32[1,216]{1,0:T(1,128)}, u32[]{:S(2)}) copy-start(f32[1,216]{1,0:T(1,128)} %constant.1608) | copy-start | bytes 2596
  103.0 5.0 %copy-start.13 = (f32[8]{0:T(128)S(1)}, f32[8]{0:T(128)}, u32[]{:S(2)}) copy-start(f32[8]{0:T(128)} %constant.1594) | copy-start | bytes 100
  103.0 5.0 %copy-start.14 = (f32[8]{0:T(128)S(1)}, f32[8]{0:T(128)}, u32[]{:S(2)}) copy-start(f32[8]{0:T(128)} %constant.1593) | copy-start | bytes 100
  103.0 5.0 %copy-start.15 = (f32[8]{0:T(128)S(1)}, f32[8]{0:T(128)}, u32[]{:S(2)}) copy-start(f32[8]{0:T(128)} %constant.1592) | copy-start | bytes 100
  103.0 47.1 %all-to-all-start.2 = ((f32[8,1,2,128,216]{3,4,2,1,0:T(8,128)}), f32[8,1,2,128,216]{3,4,2,1,0:T(8,128)}, u32[]{:S(2)}, u32[]{:S(2)}) async-start(f32[8,1,2,128,216]{3,4,2,1,0:T(8,128)} %copy.165), calls=%async_computation.2 | async-start | bytes 3538944 | tf_op jit(solution)/shard_map/all_to_all | solution.py:240
  150.1 46.4 %all-to-all-start.1 = ((f32[8,1,2,128,216]{3,4,2,1,0:T(8,128)}), f32[8,1,2,128,216]{3,4,2,1,0:T(8,128)}, u32[]{:S(2)}, u32[]{:S(2)}) async-start(f32[8,1,2,128,216]{3,4,2,1,0:T(8,128)} %copy.152), calls=%async_computation.1 | async-start | bytes 3538944 | tf_op jit(solution)/shard_map/all_to_all | solution.py:221
  176.9 24.6 %copy-start.3 = (f32[2,8,1,8,216]{4,3,2,1,0:T(8,128)S(1)}, f32[2,8,1,8,216]{4,3,2,1,0:T(8,128)}, u32[]{:S(2)}) copy-start(f32[2,8,1,8,216]{4,3,2,1,0:T(8,128)} %get-tuple-element.20) | copy-start | bytes 331780
  176.9 24.6 %copy-start.4 = (f32[2,8,1,8,216]{4,3,2,1,0:T(8,128)S(1)}, f32[2,8,1,8,216]{4,3,2,1,0:T(8,128)}, u32[]{:S(2)}) copy-start(f32[2,8,1,8,216]{4,3,2,1,0:T(8,128)} %get-tuple-element.21) | copy-start | bytes 331780
  176.9 25.4 %copy-start = (f32[16,8,1,8,216]{4,3,2,1,0:T(8,128)S(1)}, f32[16,8,1,8,216]{4,3,2,1,0:T(8,128)}, u32[]{:S(2)}) copy-start(f32[16,8,1,8,216]{4,3,2,1,0:T(8,128)} %get-tuple-element.14) | copy-start | bytes 2654212
  176.9 25.4 %copy-start.1 = (f32[16,8,1,8,216]{4,3,2,1,0:T(8,128)S(1)}, f32[16,8,1,8,216]{4,3,2,1,0:T(8,128)}, u32[]{:S(2)}) copy-start(f32[16,8,1,8,216]{4,3,2,1,0:T(8,128)} %get-tuple-element.15) | copy-start | bytes 2654212
  196.5 35.4 %all-to-all-start.3 = ((f32[4,2,2,128,216]{3,4,2,1,0:T(8,128)}), f32[4,2,2,128,216]{3,4,2,1,0:T(8,128)}, u32[]{:S(2)}, u32[]{:S(2)}) async-start(f32[4,2,2,128,216]{3,4,2,1,0:T(8,128)} %copy.168), calls=%async_computation.3 | async-start | bytes 3538944 | tf_op jit(solution)/shard_map/all_to_all | solution.py:240
where the time goes:
time: 276 us; the launch traced here: 274 us
  Pallas kernels  123 us (45%)
  local copies, waits for them, and re-layouts  50.7 us (18%)
  other arithmetic  41.6 us (15%)
  waiting for transfers between devices  38.3 us (14%)
  starting transfers between devices  19 us (7%)
    pallas_call x8, Pallas kernels, level_call(): pl.pallas_call(kernel, grid=(count // cb, tgt // tb), in_specs=[spec(), p...  123 us
    all_to_all x2, waiting for transfers between devices, shards(): x = lax.all_to_all(x, op, split_axis=0, concat_axis=0, tiled=True)  19.5 us
    all_to_all x2, waiting for transfers between devices, shards(): y = lax.all_to_all(y, op, split_axis=0, concat_axis=0, tiled=True)  18.8 us
    transpose x4, local copies, waits for them, and re-layouts, forward_level(): return out.swapaxes(2, 3).reshape(count // 8, 2, tgt * 8, q)  12.3 us
    all_to_all x2, starting transfers between devices, shards(): x = lax.all_to_all(x, op, split_axis=0, concat_axis=0, tiled=True)  9.67 us
    all_to_all x2, starting transfers between devices, shards(): y = lax.all_to_all(y, op, split_axis=0, concat_axis=0, tiled=True)  9.38 us
    another operation x3, local copies, waits for them, and re-layouts, adjoint_level(): operand = y.reshape(count, 2, tgt // 8, 8, q).swapaxes(2, 3)  7.79 us
    mul x4, other arithmetic, turn_of(): return (sign * c, sign * (s * y))  7.19 us
  transfers between devices with their start and end apart: 4, of which 2 were waited for; matrix products, arithmetic and copies ran while one was open for 19% of the time, Pallas kernels for 22%

commit v1 on v0

--- a/solution.py
+++ b/solution.py
@@ -164,7 +164,7 @@
     )(operand, phase, *tables)
 
 
-def forward_level(x, src_off, level, medium, tables):
+def general_forward_level(x, src_off, level, medium, tables):
     count, _, tgt, q = x.shape
     phase = child_phase(src_off, count, level, medium).reshape(count // 8, 8, 2, 8, q)
     out = level_call(
@@ -173,7 +173,7 @@
     return out.swapaxes(2, 3).reshape(count // 8, 2, tgt * 8, q)
 
 
-def adjoint_level(y, src_off, level, medium, tables):
+def general_adjoint_level(y, src_off, level, medium, tables):
     count, _, tgt, q = y.shape
     phase = child_phase(src_off * 8, count * 8, level, medium).reshape(count, 8, 2, 8, q)
     operand = y.reshape(count, 2, tgt // 8, 8, q).swapaxes(2, 3)
@@ -181,7 +181,7 @@
     return out.reshape(count * 8, 2, tgt // 8, q)
 
 
-def shards(forward_weights, adjoint_weights, medium):
+def general_shards(forward_weights, adjoint_weights, medium):
     table = child_table(ORDER) / math.sqrt(8.0)
     forward_tables = split_table(table)
     adjoint_tables = split_table(table.transpose(0, 2, 1))
@@ -212,7 +212,7 @@
         x = jnp.stack([re * c - im * s, re * s + im * c], axis=1)
         for op in plan:
             if op == "level":
-                x = forward_level(x, src, level, medium, forward_tables)
+                x = general_forward_level(x, src, level, medium, forward_tables)
                 src, tgt, level = src // 8, tgt * 8, level + 1
             else:
                 n = sizes[op]
@@ -231,7 +231,7 @@
         y = jnp.stack([re * c - im * s, re * s + im * c], axis=1)
         for op in reversed(plan):
             if op == "level":
-                y = adjoint_level(y, src, level - 1, medium, adjoint_tables)
+                y = general_adjoint_level(y, src, level - 1, medium, adjoint_tables)
                 src, tgt, level = src * 8, tgt // 8, level - 1
             else:
                 n = sizes[op]
@@ -249,6 +249,451 @@
     return f.reshape(f.shape[0], -1), b.reshape(b.shape[0], b.shape[1], -1)
 
 
+HALF = Q // 2
+ROWS = 512
+
+
+def lane_points():
+    t = np.arange(HALF)
+    return t, (ORDER - 1 - t // ORDER**2) * ORDER**2 + t % ORDER**2
+
+
+def parity_tables():
+    t, m = lane_points()
+    table = child_table(ORDER) / math.sqrt(8.0)
+    out = np.zeros((4, 2, 256, 128))
+    for e in range(4):
+        rows = np.zeros((256, Q))
+        rows[:HALF] = table[e][t]
+        rows[128 : 128 + HALF] = table[e][m]
+        for s, sign in enumerate((1.0, -1.0)):
+            out[e, s, :, :HALF] = 0.5 * (rows[:, t] + sign * rows[:, m])
+    high = out.astype(ml_dtypes.bfloat16)
+    return high, (out - high.astype(np.float64)).astype(ml_dtypes.bfloat16)
+
+
+def forward_parity_table():
+    high, low = parity_tables()
+    return jnp.asarray(np.concatenate([high, low], axis=-1))
+
+
+def adjoint_parity_table():
+    parts = [np.concatenate([x.swapaxes(-1, -2)] * 2, axis=2) for x in parity_tables()]
+    return jnp.asarray(np.stack(parts, axis=2))
+
+
+def grid_lanes():
+    t, m = lane_points()
+    g = cheb_points(ORDER).astype(np.float32)
+    full = (np.repeat(g, ORDER * ORDER), np.tile(np.repeat(g, ORDER), ORDER), np.tile(g, ORDER**2))
+    out = np.zeros((3, 256), np.float32)
+    for d in range(3):
+        out[d, :HALF], out[d, 128 : 128 + HALF] = full[d][t], full[d][m]
+    return out
+
+
+def lane_slopes(src_off, count, groups, medium):
+    side = band / float(2**groups)
+    grid = grid_lanes()
+    corner = box_coords(src_off + jnp.arange(count, dtype=jnp.int32), groups)
+    pts = [side * (c[:, None] + o[None, :]) for c, o in zip(corner, grid)]
+    radius = jnp.sqrt(pts[0] * pts[0] + pts[1] * pts[1] + pts[2] * pts[2])
+    return [p + medium[d + 1] * radius for d, p in enumerate(pts)], medium[0] * radius
+
+
+def level_phase(src_off, count, level, medium):
+    slopes, _ = lane_slopes(src_off, count, LEVELS - level, medium)
+    k = np.arange(4)
+    u = 0.0
+    for bits, a in zip((k // 4, k // 2 % 2, k % 2), slopes):
+        step = ((bits - 0.5) / 2.0 ** (level + 2)).astype(np.float32)
+        u = u + step[None, :, None] * a[:, None, :]
+    return jnp.concatenate(turn_of(u), axis=1)
+
+
+def first_phase(src_off, count, medium):
+    slopes, u = lane_slopes(src_off, count, LEVELS, medium)
+    k = np.arange(8)
+    u = u[:, None, :]
+    for bits, a in zip((k // 4, k // 2 % 2, k % 2), slopes):
+        u = u + ((bits + 0.5) / 2.0).astype(np.float32)[None, :, None] * a[:, None, :]
+    return jnp.stack(turn_of(u), axis=1)
+
+
+def last_phase(tgt_off, count, medium):
+    slopes, base = lane_slopes(jnp.int32(0), 1, 0, medium)
+    coords = box_coords(tgt_off // 64 + jnp.arange(count // 64, dtype=jnp.int32), LEVELS - 1)
+    u = base
+    for c, a in zip(coords, slopes):
+        u = u + ((c + 0.5) / 2.0 ** (LEVELS - 1))[:, None] * a
+    high = jnp.stack(turn_of(u))[:, :, None, :]
+    v = 0.0
+    for c, a in zip(box_coords(jnp.arange(64, dtype=jnp.int32), 2), slopes):
+        v = v + ((c - 1.5) / 2.0 ** (LEVELS + 1))[:, None] * a
+    return high, jnp.stack(turn_of(v))
+
+
+def split(x):
+    high = x.astype(jnp.bfloat16)
+    return high, (x - high.astype(jnp.float32)).astype(jnp.bfloat16)
+
+
+def dot(a, b):
+    return jnp.dot(a, b, preferred_element_type=jnp.float32)
+
+
+def forward_block(load, phase, table_ref, store, pb, kps, tgt):
+    total = [None, None]
+    for ep in range(4):
+        parts = ([], [])
+        for p in range(pb):
+            a, b = load(p, ep), load(p, ep + 4)
+            for kp in kps:
+                (ca, sa), (cb, sb) = phase(p, ep, kp), phase(p, ep + 4, kp)
+                for c, wa, wb in ((0, ca, cb), (1, sa, sb), (0, sa, sb), (1, ca, cb)):
+                    va = [a[c][t] * wa[t] for t in range(2)]
+                    vb = [b[c][t] * wb[t] for t in range(2)]
+                    parts[0].append(jnp.concatenate([va[0] + vb[1], va[1] + vb[0]], axis=1))
+                    parts[1].append(jnp.concatenate([va[0] - vb[1], va[1] - vb[0]], axis=1))
+        for s in range(2):
+            high, low = split(jnp.concatenate(parts[s], axis=0))
+            table = table_ref[ep, s]
+            r = dot(high, table) + dot(low, table)
+            total[s] = r if total[s] is None else total[s] + r
+    even, odd = (x[:, :128] + x[:, 128:] for x in total)
+    n = 0
+    for p in range(pb):
+        for kp in kps:
+            q = []
+            for _ in range(4):
+                rows = slice(n, n + tgt)
+                q.append((even[rows] + odd[rows], even[rows] - odd[rows]))
+                n += tgt
+            for t in range(2):
+                rc, si, rs, ci = (x[t] for x in q)
+                store(p, kp, t, (rc - si, rs + ci))
+                store(p, 7 - kp, t, (rc + si, ci - rs))
+
+
+def phase_of(w_ref):
+    def phase(s, kp):
+        return [[w_ref[s, i : i + 1, t * 128 : t * 128 + 128] for t in range(2)] for i in (kp, 4 + kp)]
+
+    return phase
+
+
+def forward_level(load, w_ref, table_ref, y_ref, parents, tgt):
+    pb, kb = min(parents, max(1, ROWS // (16 * tgt))), min(4, max(1, ROWS // (4 * tgt)))
+    phase = phase_of(w_ref)
+    for g in range(0, 4, kb):
+
+        def body(i, carry):
+            def store(p, k, t, values):
+                for c in range(2):
+                    y_ref[i * pb + p, c, t, k * tgt : (k + 1) * tgt] = values[c]
+
+            source = lambda p, e: (i * pb + p) * 8 + e
+            forward_block(
+                lambda p, e: load(source(p, e)),
+                lambda p, e, kp: phase(source(p, e), kp),
+                table_ref, store, pb, range(g, g + kb), tgt,
+            )
+            return carry
+
+        lax.fori_loop(0, parents // pb, body, 0)
+
+
+def adjoint_block(load, phase, table_ref, store, pb, tgt):
+    parts = ([], [])
+    for p in range(pb):
+        for kp in range(4):
+            a, b = load(p, kp), load(p, 7 - kp)
+            for c, sign in ((0, 1), (1, -1), (0, -1), (1, 1)):
+                x = [a[c][t] + b[c][t] if sign > 0 else a[c][t] - b[c][t] for t in range(2)]
+                parts[0].append(x[0] + x[1])
+                parts[1].append(x[0] - x[1])
+    rows = [jnp.concatenate(split(jnp.concatenate(x, axis=0)), axis=1) for x in parts]
+    for ep in range(4):
+        even, odd = (dot(rows[s], table_ref[ep, s, 0]) + dot(rows[s], table_ref[ep, s, 1]) for s in range(2))
+        tiles = [slice(0, 128), slice(128, 256)]
+        near = [even[:, t] + odd[:, t] for t in tiles]
+        far = [even[:, t] - odd[:, t] for t in reversed(tiles)]
+        for e, z in ((ep, near), (ep + 4, far)):
+            n = 0
+            for p in range(pb):
+                out = [[None, None], [None, None]]
+                for kp in range(4):
+                    cs, sn = phase(p, e, kp)
+                    for t in range(2):
+                        q = [z[t][n + i * tgt : n + (i + 1) * tgt] for i in range(4)]
+                        re, im = q[0] * cs[t] + q[1] * sn[t], q[3] * cs[t] - q[2] * sn[t]
+                        out[0][t] = re if kp == 0 else out[0][t] + re
+                        out[1][t] = im if kp == 0 else out[1][t] + im
+                    n += 4 * tgt
+                store(p, e, out)
+
+
+def adjoint_level(y_ref, w_ref, table_ref, store, parents, tgt):
+    tb = min(tgt, 32)
+    pb, nt = min(parents, 32 // tb), tgt // tb
+    phase = phase_of(w_ref)
+
+    def body(i, carry):
+        p0, t0 = (i // nt) * pb, pl.multiple_of((i % nt) * tb, 8)
+
+        def load(p, k):
+            rows = pl.ds(pl.multiple_of(k * tgt + t0, 8), tb)
+            return [[y_ref[p0 + p, c, t, rows] for t in range(2)] for c in range(2)]
+
+        source = lambda p, e: (p0 + p) * 8 + e
+        adjoint_block(
+            load,
+            lambda p, e, kp: phase(source(p, e), kp),
+            table_ref,
+            lambda p, e, out: store(source(p, e), t0, tb, out),
+            pb, tb,
+        )
+        return carry
+
+    lax.fori_loop(0, (parents // pb) * nt, body, 0)
+
+
+def to_lanes(x):
+    out = []
+    for n in (0, Q):
+        far = [x[:, n + a : n + a + 36] for a in (180, 144, 108)] + [x[:, n : n + 20]]
+        out.append([x[:, n : n + 128], jnp.concatenate(far, axis=1)])
+    return out
+
+
+def from_lanes(x):
+    parts = []
+    for c in range(2):
+        parts += [x[c][0][:, :HALF]] + [x[c][1][:, a : a + 36] for a in (72, 36, 0)]
+    return jnp.concatenate(parts, axis=1)
+
+
+def turn(x, c, s, sign=1):
+    if sign > 0:
+        return [[x[0][t] * c[t] - x[1][t] * s[t] for t in range(2)], [x[0][t] * s[t] + x[1][t] * c[t] for t in range(2)]]
+    return [[x[0][t] * c[t] + x[1][t] * s[t] for t in range(2)], [x[1][t] * c[t] - x[0][t] * s[t] for t in range(2)]]
+
+
+def pack(groups):
+    out, rest = [], []
+    for x in groups:
+        last = x[1][1]
+        for i, y in enumerate((x[0][0], x[0][1], x[1][0])):
+            out.append(jnp.concatenate([y[:, :HALF], last[:, 20 * i : 20 * i + 20]], axis=1))
+        rest.append(last[:, 60:HALF])
+    out.append(jnp.concatenate([rest[0], rest[0][:, :16], rest[1], rest[1][:, :16]], axis=1))
+    return out
+
+
+def unpack(x):
+    groups = []
+    for g in range(2):
+        y = x[3 * g : 3 * g + 3]
+        tail = x[6][:, 64 * g : 64 * g + 48]
+        last = jnp.concatenate([v[:, HALF:] for v in y] + [tail, tail[:, :20]], axis=1)
+        groups.append([[y[0], y[1]], [y[2], last]])
+    return groups
+
+
+def join_rows(groups):
+    return [[jnp.concatenate([g[c][t] for g in groups], axis=0) for t in range(2)] for c in range(2)]
+
+
+def forward_first(geo, x_ref, p0_ref, w0_ref, w1_ref, table_ref, o_ref, x_buf, y0_buf, y1_buf):
+    D, m, T, slot = geo
+
+    def first(i, carry):
+        for j in range(4):
+            s = i * 4 + j
+            cs, sn = ([p0_ref[s, n, :, t * 128 : t * 128 + 128] for t in range(2)] for n in range(2))
+            x = turn(to_lanes(x_ref[s]), cs, sn)
+            for c in range(2):
+                for t in range(2):
+                    x_buf[s, c, t] = x[c][t]
+        return carry
+
+    lax.fori_loop(0, 16 * m, first, 0)
+    read = lambda ref: lambda s: [[ref[s, c, t] for t in range(2)] for c in range(2)]
+    forward_level(read(x_buf), w0_ref, table_ref, y0_buf, 8 * m, 8)
+    forward_level(read(y0_buf), w1_ref, table_ref, y1_buf, m, 64)
+
+    def send(i, carry):
+        for r in range(4):
+            d = i * 4 + r
+            for p in range(m):
+                groups = []
+                for g in range(T // 8):
+                    box = d * (T // 8) + g
+                    rows = pl.ds((box % 8) * 8 + box // 8, 8, stride=64)
+                    groups.append([[y1_buf[p, c, t, rows] for t in range(2)] for c in range(2)])
+                for n, v in enumerate(pack(groups)):
+                    o_ref[slot(d), p, n] = v
+        return carry
+
+    lax.fori_loop(0, D // 4, send, 0)
+
+
+def forward_second(geo, x_ref, w2_ref, w3_ref, eh_ref, el_ref, table_ref, o_ref, y2_buf, y3_buf):
+    D, m, T, slot = geo
+
+    def load(s):
+        i = slot(s // m)
+        return join_rows(unpack([x_ref[i, s % m, n] for n in range(7)]))
+
+    forward_level(load, w2_ref, table_ref, y2_buf, 8, T)
+    read = lambda ref: lambda s: [[ref[s, c, t] for t in range(2)] for c in range(2)]
+    forward_level(read(y2_buf), w3_ref, table_ref, y3_buf, 1, 8 * T)
+
+    def last(a, carry):
+        hc, hs = ([eh_ref[n, a, :, t * 128 : t * 128 + 128] for t in range(2)] for n in range(2))
+        for k in range(8):
+            rows = pl.ds(k * T + a, 8, stride=8 * T)
+            x = [[y3_buf[0, c, t, rows] for t in range(2)] for c in range(2)]
+            lc, ls = ([el_ref[n, k * 8 : k * 8 + 8, t * 128 : t * 128 + 128] for t in range(2)] for n in range(2))
+            x = turn(turn(x, lc, ls, -1), hc, hs, -1)
+            o_ref[pl.ds(pl.multiple_of(a * 64 + k * 8, 8), 8), :] = from_lanes(x)
+        return carry
+
+    lax.fori_loop(0, T, last, 0)
+
+
+def adjoint_first(geo, y_ref, w2_ref, w3_ref, eh_ref, el_ref, table_ref, o_ref, y_buf, x3_buf):
+    D, m, T, slot = geo
+
+    def first(a, carry):
+        hc, hs = ([eh_ref[n, a, :, t * 128 : t * 128 + 128] for t in range(2)] for n in range(2))
+        for k in range(8):
+            x = to_lanes(y_ref[pl.ds(pl.multiple_of(a * 64 + k * 8, 8), 8), :])
+            lc, ls = ([el_ref[n, k * 8 : k * 8 + 8, t * 128 : t * 128 + 128] for t in range(2)] for n in range(2))
+            x = turn(turn(x, lc, ls), hc, hs)
+            for c in range(2):
+                for t in range(2):
+                    y_buf[0, c, t, pl.ds(k * T + a, 8, stride=8 * T)] = x[c][t]
+        return carry
+
+    lax.fori_loop(0, T, first, 0)
+
+    def keep(s, t0, tb, out):
+        for c in range(2):
+            for t in range(2):
+                x3_buf[s, c, t, pl.ds(t0, tb)] = out[c][t]
+
+    adjoint_level(y_buf, w3_ref, table_ref, keep, 1, 8 * T)
+
+    def send(s, t0, tb, out):
+        groups = [[[out[c][t][g * 8 : g * 8 + 8] for t in range(2)] for c in range(2)] for g in range(T // 8)]
+        for n, v in enumerate(pack(groups)):
+            o_ref[slot(s // m), s % m, n] = v
+
+    adjoint_level(x3_buf, w2_ref, table_ref, send, 8, T)
+
+
+def adjoint_second(geo, y_ref, p0_ref, w0_ref, w1_ref, table_ref, o_ref, y_buf, x1_buf, x0_buf):
+    D, m, T, slot = geo
+
+    def first(i, carry):
+        for r in range(4):
+            d = i * 4 + r
+            for p in range(m):
+                for g, x in enumerate(unpack([y_ref[slot(d), p, n] for n in range(7)])):
+                    box = d * (T // 8) + g
+                    rows = pl.ds((box % 8) * 8 + box // 8, 8, stride=64)
+                    for c in range(2):
+                        for t in range(2):
+                            y_buf[p, c, t, rows] = x[c][t]
+        return carry
+
+    lax.fori_loop(0, D // 4, first, 0)
+
+    def keep(s, t0, tb, out):
+        for c in range(2):
+            for t in range(2):
+                x1_buf[s, c, t, pl.ds(t0, tb)] = out[c][t]
+
+    adjoint_level(y_buf, w1_ref, table_ref, keep, m, 64)
+
+    def last(s, t0, tb, out):
+        cs, sn = ([p0_ref[s, n, :, t * 128 : t * 128 + 128] for t in range(2)] for n in range(2))
+        out = turn(out, cs, sn, -1)
+        for c in range(2):
+            for t in range(2):
+                x0_buf[c, t, pl.ds(pl.multiple_of(s * 8, 8), 8)] = out[c][t]
+
+    adjoint_level(x1_buf, w0_ref, table_ref, last, 8 * m, 8)
+
+    def turn_rows(i, carry):
+        for a in range(8):
+            rows = pl.ds(i * 64 + a, 8, stride=8)
+            x = [[x0_buf[c, t, rows] for t in range(2)] for c in range(2)]
+            o_ref[a, pl.ds(pl.multiple_of(i * 8, 8), 8), :] = from_lanes(x)
+        return carry
+
+    lax.fori_loop(0, 8 * m, turn_rows, 0)
+
+
+def vmem_call(kernel, out_shape, scratch, *args):
+    spec = pl.BlockSpec(memory_space=pltpu.VMEM)
+    return pl.pallas_call(
+        kernel,
+        in_specs=[spec] * len(args),
+        out_specs=spec,
+        out_shape=jax.ShapeDtypeStruct(out_shape, jnp.float32),
+        scratch_shapes=[pltpu.VMEM(s, jnp.float32) for s in scratch],
+        compiler_params=pltpu.CompilerParams(vmem_limit_bytes=56 * 1024 * 1024),
+    )(*args)
+
+
+def one_exchange_shards(forward_weights, adjoint_weights, medium):
+    nx, ny = lax.axis_size("sx"), lax.axis_size("sy")
+    ix, iy = lax.axis_index("sx"), lax.axis_index("sy")
+    D, S, R = nx * ny, forward_weights.shape[0], adjoint_weights.shape[0]
+    m, T = S // 64, R // 64
+    natural = lambda d: d
+    swapped = lambda d: (d % nx) * ny + d // nx
+    swapped_back = lambda d: (d % ny) * nx + d // ny
+    src, tgt = (iy * nx + ix) * S, (ix * ny + iy) * R
+    forward_table, adjoint_table = forward_parity_table(), adjoint_parity_table()
+    p0 = first_phase(src, S, medium)
+    w0 = level_phase(src, S, 0, medium)
+    w1 = level_phase(src // 8, S // 8, 1, medium)
+    w2 = level_phase(jnp.int32(0), 64, 2, medium)
+    w3 = level_phase(jnp.int32(0), 8, 3, medium)
+    eh, el = last_phase(tgt, R, medium)
+    wire = (D, m, 7, 8, 128)
+    data = lambda s, t: (s, 2, 2, t, 128)
+    x = vmem_call(
+        lambda *a: forward_first((D, m, T, natural), *a), wire,
+        [data(S, 8), data(8 * m, 64), data(m, 512)], forward_weights, p0, w0, w1, forward_table,
+    )
+    x = lax.all_to_all(x, ("sx", "sy"), split_axis=0, concat_axis=0, tiled=True)
+    y = vmem_call(
+        lambda *a: adjoint_first((D, m, T, swapped), *a), wire,
+        [data(1, 64 * T), data(8, 8 * T)], adjoint_weights, w2, w3, eh, el, adjoint_table,
+    )
+    y = lax.all_to_all(y, ("sx", "sy"), split_axis=0, concat_axis=0, tiled=True)
+    f = vmem_call(
+        lambda *a: forward_second((D, m, T, swapped), *a), (R, 2 * Q),
+        [data(8, 8 * T), data(1, 64 * T)], x, w2, w3, eh, el, forward_table,
+    )
+    b = vmem_call(
+        lambda *a: adjoint_second((D, m, T, natural), *a), (8, S, 2 * Q),
+        [data(m, 512), data(8 * m, 64), (2, 2, S * 8, 128)], y, p0, w0, w1, adjoint_table,
+    )
+    return f, b
+
+
+def shards(forward_weights, adjoint_weights, medium):
+    devices = lax.axis_size("sx") * lax.axis_size("sy")
+    S, R = forward_weights.shape[0], adjoint_weights.shape[0]
+    one = S % 64 == 0 and (S // 64) * devices == 64 and R == 1024 and forward_weights.shape[2] == 2 * Q
+    return (one_exchange_shards if one else general_shards)(forward_weights, adjoint_weights, medium)
+
+
 def solution(mesh):
     in_specs = (P(("sy", "sx"), None, None), P(("sx", "sy"), None), P())
     out_specs = (P(("sx", "sy"), None), P(None, ("sy", "sx"), None))

time: 276 us -> 161 us (0.58)
  Pallas kernels: 123 us -> 76.2 us
  local copies, waits for them, and re-layouts: 50.7 us -> 13.8 us
  other arithmetic: 41.6 us -> 21.5 us
  starting transfers between devices: 19 us -> 10.9 us
    pallas_call x8 -> x4, Pallas kernels: 123 us -> 76.2 us  [vmem_call(): pl.pallas_call(kernel, in_specs=[spec] * len(args), out_specs=spec, out_s...]
    transpose x7 -> x0, local copies, waits for them, and re-layouts: 17.6 us -> none  [the longest x4 12.3 us: forward_level(): return out.swapaxes(2, 3).reshape(count // 8, 2, tgt * 8, q)]
    another operation x7 -> x0, local copies, waits for them, and re-layouts: 17 us -> none  [the longest x3 7.79 us: adjoint_level(): operand = y.reshape(count, 2, tgt // 8, 8, q).swapaxes(2, 3)]
    add x4 -> x0, other arithmetic: 8.44 us -> none  [the longest x3 6.59 us: point_slopes(): p + medium[d + 1] * radius]
    all_to_all x4 -> x2, starting transfers between devices: 19 us -> 10.9 us  [the longest x1 7.5 us: one_exchange_shards(): x = lax.all_to_all(x, ('sx', 'sy'), split_axis=0, concat_axis=0, tiled=True)]
    another operation x8 -> x3, other arithmetic: 9.31 us -> 2.16 us  [the longest x1 1.49 us: first_phase(): return jnp.stack(turn_of(u), axis=1)]
    all_to_all x3 -> x0, local copies, waits for them, and re-layouts: 6.62 us -> none  [the longest x2 4.74 us: shards(): x = lax.all_to_all(x, op, split_axis=0, concat_axis=0, tiled=True)]
    unnamed x74 -> x42, local copies, waits for them, and re-layouts: 5.12 us -> 11.7 us
  transfers between devices with their start and end apart: 4 -> 2, of which waited for: 2 -> 2; matrix products, arithmetic and copies ran while one was open for 19% -> 10% of each run, Pallas kernels for 22% -> 22%
where the time goes in v1:
time: 161 us; the launch traced here: 160 us
  Pallas kernels  76.2 us (47%)
  waiting for transfers between devices  36.8 us (23%)
  other arithmetic  21.5 us (13%)
  local copies, waits for them, and re-layouts  13.8 us (9%)
  starting transfers between devices  10.9 us (7%)
    pallas_call x4, Pallas kernels, vmem_call(): pl.pallas_call(kernel, in_specs=[spec] * len(args), out_specs=spec, out_s...  76.2 us
    all_to_all x1, waiting for transfers between devices, one_exchange_shards(): y = lax.all_to_all(y, ('sx', 'sy'), split_axis=0, concat_axis=0, tiled=True)  25.3 us
    unnamed x42, local copies, waits for them, and re-layouts  11.7 us
    all_to_all x1, waiting for transfers between devices, one_exchange_shards(): x = lax.all_to_all(x, ('sx', 'sy'), split_axis=0, concat_axis=0, tiled=True)  11.5 us
    mul x4, other arithmetic, level_phase(): u = u + step[None, :, None] * a[:, None, :]  8.73 us
    all_to_all x1, starting transfers between devices, one_exchange_shards(): x = lax.all_to_all(x, ('sx', 'sy'), split_axis=0, concat_axis=0, tiled=True)  7.5 us
    mul x7, other arithmetic, turn_of(): return (sign * c, sign * (s * y))  4.35 us
    all_to_all x1, starting transfers between devices, one_exchange_shards(): y = lax.all_to_all(y, ('sx', 'sy'), split_axis=0, concat_axis=0, tiled=True)  3.44 us
  transfers between devices with their start and end apart: 2, of which 2 were waited for; matrix products, arithmetic and copies ran while one was open for 10% of the time, Pallas kernels for 22%

profile of v1, /device:TPU:0, one launch (start us, length us, event | category | flops | bytes accessed | tf_op | source)
XLA Modules:
  0.0 160.2 jit_solution(11380231749142665730)
XLA Ops:
  0.6 0.0 copy-start.1
  0.6 0.0 copy-start.2
  0.7 0.0 copy-start.3
  0.7 0.0 copy-start.12
  0.7 0.0 copy-start.13
  0.9 1.5 fusion.106
  2.4 0.0 copy-start.8
  2.4 0.0 copy-start.9
  2.4 3.1 %copy.50.a_0_ = f32[128,8,432]{2,1,0:T(8,128)} copy(f32[128,8,432]{0,2,1:T(8,128)} %param.38) | data formatting | bytes 3538944 | tf_op args[0]
  5.5 0.0 copy-done.1
  5.5 0.0 copy-done.2
  5.5 0.0 copy-done.3
  5.5 2.0 %fusion.36 = (f32[16,256]{1,0:T(8,128)S(1)}, f32[16,256]{1,0:T(8,128)S(1)}, f32[16,256]{1,0:T(8,128)S(1)}) fusion(f32[256]{0:T(256)S(1)} %copy-done.1, f32[16]{0:T(128)S(1)} %get-tuple-element.45, f32[256]{0:T(256)S(1)} %copy-done.2, f32[16]{0:T(128)S(1)} %fusion.102, f32[]{:T(128)} %bitcast.1, f32[256]{0:T(256)S(1)} %copy-done.3, ...), kind=kLoop, calls=%fused_computation.126 | loop fusion | flops 61440 | bytes 52428 | tf_op jit(solution)/shard_map/mul | solution.py:310
  7.4 0.0 copy-done.12
  7.5 0.0 copy-done.13
  7.5 0.2 add_multiply_fusion.9
  7.7 0.7 pad_maximum_fusion.3.a_3_
  8.4 0.0 copy-start.16
  8.4 0.0 copy-start.17
  8.4 0.0 copy-start.18
  8.4 2.8 %broadcast_multiply_fusion = (f32[128,256]{1,0:T(8,128)S(1)}, f32[128,256]{1,0:T(8,128)S(1)}, f32[128,256]{1,0:T(8,128)S(1)}, f32[128,256]{1,0:T(8,128)S(1)}, f32[128,256]{1,0:T(8,128)S(1)}) fusion(f32[256]{0:T(256)S(1)} %copy-done.1, f32[128]{0:T(128)S(1)} %get-tuple-element.43, f32[256]{0:T(256)S(1)} %copy-done.2, f32[128]{0:T(128)S(1)} %fusion.105, ...), kind=kLoop, calls=%fused_computation.60 | loop fusion | flops 622592 | bytes 659984 | tf_op jit(solution)/shard_map/mul | solution.py:310
  11.2 0.0 copy-done.8
  11.2 0.0 copy-done.9
  11.2 1.4 add_multiply_fusion
  12.6 1.2 pad_maximum_fusion.1.a_2_
  13.8 0.0 copy-done.16
  13.8 0.0 copy-done.17
  13.8 0.0 copy-done.18
  13.8 1.5 fusion.6
  15.3 1.5 pad_maximum_fusion.a_1_
  16.8 21.8 %shard_map.365 = f32[32,2,7,8,128]{4,3,2,1,0:T(8,128)} custom-call(f32[128,8,432]{2,1,0:T(8,128)} %copy.50.a_0_, f32[128,2,8,256]{3,2,1,0:T(8,128)} %pad_maximum_fusion.a_1_, f32[128,8,256]{2,1,0:T(8,128)} %pad_maximum_fusion.1.a_2_, f32[16,8,256]{2,1,0:T(8,128)} %pad_maximum_fusion.3.a_3_, bf16[4,2,256,256]{3,2,1,0:T(8,128)(2,1)} %constant.854.clone.a_4_.a_5_), custom_call_target="tpu_custom_call" | custom-call | tf_op jit(solution)/shard_map/pallas_call | solution.py:641
  38.6 0.0 copy-start.4
  38.6 7.5 %all-to-all-start = ((f32[32,2,7,8,128]{4,3,2,1,0:T(8,128)}), f32[32,2,7,8,128]{4,3,2,1,0:T(8,128)S(1)}, u32[]{:S(2)}, u32[]{:S(2)}) async-start(f32[32,2,7,8,128]{4,3,2,1,0:T(8,128)} %shard_map.365), calls=%async_computation | async-start | bytes 3670016 | tf_op jit(solution)/shard_map/all_to_all | solution.py:673
  46.1 0.0 copy-start.10
  46.1 0.0 copy-start.11
  46.3 0.0 copy-done.4
  46.3 0.0 copy-done.5
  46.3 0.0 copy-done.6
  46.3 0.0 copy-done.7
  46.3 2.5 %broadcast_multiply_fusion.1 = (f32[1,256]{1,0:T(1,128)S(1)}, f32[1,256]{1,0:T(1,128)S(1)}, f32[1,256]{1,0:T(1,128)S(1)}, f32[1,256]{1,0:T(1,128)S(1)}) fusion(f32[1,256]{1,0:T(1,128)S(1)} %copy-done.7, f32[]{:T(128)} %bitcast, f32[1,256]{1,0:T(1,128)S(1)} %copy-done.4, f32[]{:T(128)} %bitcast.3, f32[1,256]{1,0:T(1,128)S(1)} %copy-done.5, f32[]{:T(128)} %bitcast.2, ...), kind=kLoop, calls=%fused_computation.416 | loop fusion | flops 1792 | bytes 8208 | tf_op jit(solution)/shard_map/mul | solution.py:301
  48.8 0.1 fusion.43
  49.0 0.6 broadcast_in_dim.2.a_3_
  49.6 2.9 %copy.57.a_0_ = f32[1024,432]{1,0:T(8,128)} copy(f32[1024,432]{0,1:T(8,128)} %param.39) | data formatting | bytes 3538944 | tf_op args[1]
  52.6 2.0 %add_multiply_fusion.14 = (f32[8,256]{1,0:T(8,128)S(1)}, f32[8,256]{1,0:T(8,128)S(1)}, f32[8,256]{1,0:T(8,128)S(1)}) fusion(f32[256]{0:T(256)S(1)} %copy-done.1, f32[8]{0:T(128)S(1)} %get-tuple-element.49, f32[256]{0:T(256)S(1)} %copy-done.2, f32[8]{0:T(128)S(1)} %get-tuple-element.48, f32[]{:T(128)} %bitcast.1, f32[256]{0:T(256)S(1)} %copy-done.3, ...), kind=kLoop, calls=%fused_computation.152 | loop fusion | flops 36864 | bytes 27756 | tf_op jit(solution)/shard_map/mul | solution.py:310
  54.6 0.0 copy-done.10
  54.6 0.0 copy-done.11
  54.6 0.2 add_multiply_fusion.10
  54.7 0.6 pad_maximum_fusion.5.a_2_
  55.4 0.2 fusion.22
  55.6 0.7 pad_maximum_fusion.4.a_4_
  56.2 2.0 %add_multiply_fusion.5 = (f32[64,256]{1,0:T(8,128)S(1)}, f32[64,256]{1,0:T(8,128)S(1)}, f32[64,256]{1,0:T(8,128)S(1)}) fusion(f32[256]{0:T(256)S(1)} %copy-done.1, f32[64]{0:T(128)S(1)} %get-tuple-element.47, f32[256]{0:T(256)S(1)} %copy-done.2, f32[64]{0:T(128)S(1)} %fusion.100, f32[]{:T(128)} %bitcast.1, f32[256]{0:T(256)S(1)} %copy-done.3, ...), kind=kLoop, calls=%fused_computation.86 | loop fusion | flops 294912 | bytes 200460 | tf_op jit(solution)/shard_map/mul | solution.py:310
  58.2 0.0 copy-done.14
  58.3 0.0 copy-done.15
  58.3 0.8 add_multiply_fusion.1
  59.0 0.9 pad_maximum_fusion.2.a_1_
  59.9 18.9 %shard_map.367 = f32[32,2,7,8,128]{4,3,2,1,0:T(8,128)} custom-call(f32[1024,432]{1,0:T(8,128)} %copy.57.a_0_, f32[64,8,256]{2,1,0:T(8,128)} %pad_maximum_fusion.2.a_1_, f32[8,8,256]{2,1,0:T(8,128)} %pad_maximum_fusion.5.a_2_, f32[2,16,1,256]{3,2,1,0:T(1,128)} %broadcast_in_dim.2.a_3_, f32[2,64,256]{2,1,0:T(8,128)} %pad_maximum_fusion.4.a_4_, ...), custom_call_target="tpu_custom_call" | custom-call | tf_op jit(solution)/shard_map/pallas_call | solution.py:641
  78.8 11.5 %all-to-all-done.a_0_ = f32[32,2,7,8,128]{4,3,2,1,0:T(8,128)S(1)} async-done(((f32[32,2,7,8,128]{4,3,2,1,0:T(8,128)}), f32[32,2,7,8,128]{4,3,2,1,0:T(8,128)S(1)}, u32[]{:S(2)}, u32[]{:S(2)}) %all-to-all-start) | async-done | bytes 1835040 | tf_op jit(solution)/shard_map/all_to_all | solution.py:673
  90.3 3.4 %all-to-all-start.1 = ((f32[32,2,7,8,128]{4,3,2,1,0:T(8,128)}), f32[32,2,7,8,128]{4,3,2,1,0:T(8,128)}, u32[]{:S(2)}, u32[]{:S(2)}) async-start(f32[32,2,7,8,128]{4,3,2,1,0:T(8,128)} %shard_map.367), calls=%async_computation.1 | async-start | bytes 3670016 | tf_op jit(solution)/shard_map/all_to_all | solution.py:678
  93.8 0.0 copy-done
  93.8 16.3 %shard_map.366 = f32[1024,432]{1,0:T(8,128)} custom-call(f32[32,2,7,8,128]{4,3,2,1,0:T(8,128)} %copy-done, f32[64,8,256]{2,1,0:T(8,128)} %pad_maximum_fusion.2.a_1_, f32[8,8,256]{2,1,0:T(8,128)} %pad_maximum_fusion.5.a_2_, f32[2,16,1,256]{3,2,1,0:T(1,128)} %broadcast_in_dim.2.a_3_, f32[2,64,256]{2,1,0:T(8,128)} %pad_maximum_fusion.4.a_4_, ...), custom_call_target="tpu_custom_call" | custom-call | tf_op jit(solution)/shard_map/pallas_call | solution.py:641
  110.1 2.8 %copy.58 = f32[1024,432]{0,1:T(8,128)} copy(f32[1024,432]{1,0:T(8,128)} %shard_map.366) | data formatting | bytes 3538944
  112.8 25.3 %all-to-all-done.1.a_0_ = f32[32,2,7,8,128]{4,3,2,1,0:T(8,128)} async-done(((f32[32,2,7,8,128]{4,3,2,1,0:T(8,128)}), f32[32,2,7,8,128]{4,3,2,1,0:T(8,128)}, u32[]{:S(2)}, u32[]{:S(2)}) %all-to-all-start.1) | async-done | bytes 1835040 | tf_op jit(solution)/shard_map/all_to_all | solution.py:678
  138.1 19.3 %shard_map.368 = f32[8,128,432]{2,1,0:T(8,128)} custom-call(f32[32,2,7,8,128]{4,3,2,1,0:T(8,128)} %all-to-all-done.1.a_0_, f32[128,2,8,256]{3,2,1,0:T(8,128)} %pad_maximum_fusion.a_1_, f32[128,8,256]{2,1,0:T(8,128)} %pad_maximum_fusion.1.a_2_, f32[16,8,256]{2,1,0:T(8,128)} %pad_maximum_fusion.3.a_3_, bf16[4,2,2,256,256]{4,3,2,1,0:T(8,128)(2,1)} %constant.855.clone.a_5_.a_4_), custom_call_target="tpu_custom_call" | custom-call | tf_op jit(solution)/shard_map/pallas_call | solution.py:641
  157.4 2.8 %copy.59 = f32[8,128,432]{1,2,0:T(8,128)} copy(f32[8,128,432]{2,1,0:T(8,128)} %shard_map.368) | data formatting | bytes 3538944
  (19 shorter events, 0.3 us)
Async XLA Ops:
  0.6 4.8 %copy-start.1 = (f32[256]{0:T(256)S(1)}, f32[256]{0:T(256)}, u32[]{:S(2)}) copy-start(f32[256]{0:T(256)} %constant.876) | copy-start | bytes 3076
  0.6 4.8 %copy-start.2 = (f32[256]{0:T(256)S(1)}, f32[256]{0:T(256)}, u32[]{:S(2)}) copy-start(f32[256]{0:T(256)} %constant.875) | copy-start | bytes 3076
  0.7 4.8 %copy-start.3 = (f32[256]{0:T(256)S(1)}, f32[256]{0:T(256)}, u32[]{:S(2)}) copy-start(f32[256]{0:T(256)} %constant.874) | copy-start | bytes 3076
  0.7 6.8 %copy-start.12 = (f32[4]{0:T(128)S(1)}, f32[4]{0:T(128)}, u32[]{:S(2)}) copy-start(f32[4]{0:T(128)} %constant.883) | copy-start | bytes 52
  0.7 6.8 %copy-start.13 = (f32[4]{0:T(128)S(1)}, f32[4]{0:T(128)}, u32[]{:S(2)}) copy-start(f32[4]{0:T(128)} %constant.882) | copy-start | bytes 52
  2.4 8.8 %copy-start.8 = (f32[4]{0:T(128)S(1)}, f32[4]{0:T(128)}, u32[]{:S(2)}) copy-start(f32[4]{0:T(128)} %constant.881) | copy-start | bytes 52
  2.4 8.8 %copy-start.9 = (f32[4]{0:T(128)S(1)}, f32[4]{0:T(128)}, u32[]{:S(2)}) copy-start(f32[4]{0:T(128)} %constant.880) | copy-start | bytes 52
  8.4 5.4 %copy-start.16 = (f32[8]{0:T(128)S(1)}, f32[8]{0:T(128)}, u32[]{:S(2)}) copy-start(f32[8]{0:T(128)} %constant.879) | copy-start | bytes 100
  8.4 5.4 %copy-start.17 = (f32[8]{0:T(128)S(1)}, f32[8]{0:T(128)}, u32[]{:S(2)}) copy-start(f32[8]{0:T(128)} %constant.878) | copy-start | bytes 100
  8.4 5.4 %copy-start.18 = (f32[8]{0:T(128)S(1)}, f32[8]{0:T(128)}, u32[]{:S(2)}) copy-start(f32[8]{0:T(128)} %constant.877) | copy-start | bytes 100
  38.6 7.7 %copy-start.4 = (f32[1,256]{1,0:T(1,128)S(1)}, f32[1,256]{1,0:T(1,128)}, u32[]{:S(2)}) copy-start(f32[1,256]{1,0:T(1,128)} %constant.900) | copy-start | bytes 3076
  38.6 7.7 %copy-start.5 = (f32[1,256]{1,0:T(1,128)S(1)}, f32[1,256]{1,0:T(1,128)}, u32[]{:S(2)}) copy-start(f32[1,256]{1,0:T(1,128)} %constant.899) | copy-start | bytes 3076
  38.6 7.7 %copy-start.6 = (f32[1,256]{1,0:T(1,128)S(1)}, f32[1,256]{1,0:T(1,128)}, u32[]{:S(2)}) copy-start(f32[1,256]{1,0:T(1,128)} %constant.898) | copy-start | bytes 3076
  38.6 7.7 %copy-start.7 = (f32[1,256]{1,0:T(1,128)S(1)}, f32[1,256]{1,0:T(1,128)}, u32[]{:S(2)}) copy-start(f32[1,256]{1,0:T(1,128)} %constant.897) | copy-start | bytes 3076
  38.6 51.7 %all-to-all-start = ((f32[32,2,7,8,128]{4,3,2,1,0:T(8,128)}), f32[32,2,7,8,128]{4,3,2,1,0:T(8,128)S(1)}, u32[]{:S(2)}, u32[]{:S(2)}) async-start(f32[32,2,7,8,128]{4,3,2,1,0:T(8,128)} %shard_map.365), calls=%async_computation | async-start | bytes 3670016 | tf_op jit(solution)/shard_map/all_to_all | solution.py:673
  46.1 8.4 %copy-start.10 = (f32[4]{0:T(128)S(1)}, f32[4]{0:T(128)}, u32[]{:S(2)}) copy-start(f32[4]{0:T(128)} %constant.887) | copy-start | bytes 52
  46.1 8.4 %copy-start.11 = (f32[4]{0:T(128)S(1)}, f32[4]{0:T(128)}, u32[]{:S(2)}) copy-start(f32[4]{0:T(128)} %constant.886) | copy-start | bytes 52
  49.6 8.7 %copy-start.14 = (f32[4]{0:T(128)S(1)}, f32[4]{0:T(128)}, u32[]{:S(2)}) copy-start(f32[4]{0:T(128)} %constant.885) | copy-start | bytes 52
  49.6 8.7 %copy-start.15 = (f32[4]{0:T(128)S(1)}, f32[4]{0:T(128)}, u32[]{:S(2)}) copy-start(f32[4]{0:T(128)} %constant.884) | copy-start | bytes 52
  90.3 3.5 %copy-start = (f32[32,2,7,8,128]{4,3,2,1,0:T(8,128)}, f32[32,2,7,8,128]{4,3,2,1,0:T(8,128)S(1)}, u32[]{:S(2)}) copy-start(f32[32,2,7,8,128]{4,3,2,1,0:T(8,128)S(1)} %all-to-all-done.a_0_) | copy-start | bytes 5505028
  90.3 47.8 %all-to-all-start.1 = ((f32[32,2,7,8,128]{4,3,2,1,0:T(8,128)}), f32[32,2,7,8,128]{4,3,2,1,0:T(8,128)}, u32[]{:S(2)}, u32[]{:S(2)}) async-start(f32[32,2,7,8,128]{4,3,2,1,0:T(8,128)} %shard_map.367), calls=%async_computation.1 | async-start | bytes 3670016 | tf_op jit(solution)/shard_map/all_to_all | solution.py:678

commit v2 on v0

--- a/solution.py
+++ b/solution.py
@@ -164,7 +164,7 @@
     )(operand, phase, *tables)
 
 
-def forward_level(x, src_off, level, medium, tables):
+def general_forward_level(x, src_off, level, medium, tables):
     count, _, tgt, q = x.shape
     phase = child_phase(src_off, count, level, medium).reshape(count // 8, 8, 2, 8, q)
     out = level_call(
@@ -173,7 +173,7 @@
     return out.swapaxes(2, 3).reshape(count // 8, 2, tgt * 8, q)
 
 
-def adjoint_level(y, src_off, level, medium, tables):
+def general_adjoint_level(y, src_off, level, medium, tables):
     count, _, tgt, q = y.shape
     phase = child_phase(src_off * 8, count * 8, level, medium).reshape(count, 8, 2, 8, q)
     operand = y.reshape(count, 2, tgt // 8, 8, q).swapaxes(2, 3)
@@ -181,7 +181,7 @@
     return out.reshape(count * 8, 2, tgt // 8, q)
 
 
-def shards(forward_weights, adjoint_weights, medium):
+def general_shards(forward_weights, adjoint_weights, medium):
     table = child_table(ORDER) / math.sqrt(8.0)
     forward_tables = split_table(table)
     adjoint_tables = split_table(table.transpose(0, 2, 1))
@@ -212,7 +212,7 @@
         x = jnp.stack([re * c - im * s, re * s + im * c], axis=1)
         for op in plan:
             if op == "level":
-                x = forward_level(x, src, level, medium, forward_tables)
+                x = general_forward_level(x, src, level, medium, forward_tables)
                 src, tgt, level = src // 8, tgt * 8, level + 1
             else:
                 n = sizes[op]
@@ -231,7 +231,7 @@
         y = jnp.stack([re * c - im * s, re * s + im * c], axis=1)
         for op in reversed(plan):
             if op == "level":
-                y = adjoint_level(y, src, level - 1, medium, adjoint_tables)
+                y = general_adjoint_level(y, src, level - 1, medium, adjoint_tables)
                 src, tgt, level = src * 8, tgt // 8, level - 1
             else:
                 n = sizes[op]
@@ -249,6 +249,545 @@
     return f.reshape(f.shape[0], -1), b.reshape(b.shape[0], b.shape[1], -1)
 
 
+HALF = Q // 2
+ROWS = 512
+
+
+def lane_points():
+    t = np.arange(HALF)
+    return t, (ORDER - 1 - t // ORDER**2) * ORDER**2 + t % ORDER**2
+
+
+def parity_tables():
+    t, m = lane_points()
+    table = child_table(ORDER) / math.sqrt(8.0)
+    out = np.zeros((4, 2, 256, 128))
+    for e in range(4):
+        rows = np.zeros((256, Q))
+        rows[:HALF] = table[e][t]
+        rows[128 : 128 + HALF] = table[e][m]
+        for s, sign in enumerate((1.0, -1.0)):
+            out[e, s, :, :HALF] = 0.5 * (rows[:, t] + sign * rows[:, m])
+    high = out.astype(ml_dtypes.bfloat16)
+    return high, (out - high.astype(np.float64)).astype(ml_dtypes.bfloat16)
+
+
+def forward_parity_table():
+    high, low = parity_tables()
+    return jnp.asarray(np.concatenate([high, low], axis=-1))
+
+
+def adjoint_parity_table():
+    parts = [np.concatenate([x.swapaxes(-1, -2)] * 2, axis=2) for x in parity_tables()]
+    return jnp.asarray(np.stack(parts, axis=2))
+
+
+def split(x):
+    high = x.astype(jnp.bfloat16)
+    return high, (x - high.astype(jnp.float32)).astype(jnp.bfloat16)
+
+
+def dot(a, b):
+    return jnp.dot(a, b, preferred_element_type=jnp.float32)
+
+
+def forward_block(load, phase, table_ref, store, pb, kps, tgt):
+    total = [None, None]
+    for ep in range(4):
+        parts = ([], [])
+        for p in range(pb):
+            a, b = load(p, ep), load(p, ep + 4)
+            for kp in kps:
+                (ca, sa), (cb, sb) = phase(p, ep, kp), phase(p, ep + 4, kp)
+                for c, wa, wb in ((0, ca, cb), (1, sa, sb), (0, sa, sb), (1, ca, cb)):
+                    va = [a[c][t] * wa[t] for t in range(2)]
+                    vb = [b[c][t] * wb[t] for t in range(2)]
+                    parts[0].append(jnp.concatenate([va[0] + vb[1], va[1] + vb[0]], axis=1))
+                    parts[1].append(jnp.concatenate([va[0] - vb[1], va[1] - vb[0]], axis=1))
+        for s in range(2):
+            high, low = split(jnp.concatenate(parts[s], axis=0))
+            table = table_ref[ep, s]
+            r = dot(high, table) + dot(low, table)
+            total[s] = r if total[s] is None else total[s] + r
+    even, odd = (x[:, :128] + x[:, 128:] for x in total)
+    n = 0
+    for p in range(pb):
+        for kp in kps:
+            q = []
+            for _ in range(4):
+                rows = slice(n, n + tgt)
+                q.append((even[rows] + odd[rows], even[rows] - odd[rows]))
+                n += tgt
+            for t in range(2):
+                rc, si, rs, ci = (x[t] for x in q)
+                store(p, kp, t, (rc - si, rs + ci))
+                store(p, 7 - kp, t, (rc + si, ci - rs))
+
+
+def phase_of(w_ref, first=0):
+    def phase(s, kp):
+        return [[w_ref[t, first + s, i : i + 1] for t in range(2)] for i in (kp, 4 + kp)]
+
+    return phase
+
+
+def forward_level(load, phase, table_ref, y_ref, parents, tgt):
+    pb, kb = min(parents, max(1, ROWS // (16 * tgt))), min(4, max(1, ROWS // (4 * tgt)))
+    for g in range(0, 4, kb):
+
+        def body(i, carry):
+            def store(p, k, t, values):
+                for c in range(2):
+                    y_ref[i * pb + p, c, t, k * tgt : (k + 1) * tgt] = values[c]
+
+            source = lambda p, e: (i * pb + p) * 8 + e
+            forward_block(
+                lambda p, e: load(source(p, e)),
+                lambda p, e, kp: phase(source(p, e), kp),
+                table_ref, store, pb, range(g, g + kb), tgt,
+            )
+            return carry
+
+        lax.fori_loop(0, parents // pb, body, 0)
+
+
+def adjoint_block(load, phase, table_ref, store, pb, tgt):
+    parts = ([], [])
+    for p in range(pb):
+        for kp in range(4):
+            a, b = load(p, kp), load(p, 7 - kp)
+            for c, sign in ((0, 1), (1, -1), (0, -1), (1, 1)):
+                x = [a[c][t] + b[c][t] if sign > 0 else a[c][t] - b[c][t] for t in range(2)]
+                parts[0].append(x[0] + x[1])
+                parts[1].append(x[0] - x[1])
+    rows = [jnp.concatenate(split(jnp.concatenate(x, axis=0)), axis=1) for x in parts]
+    for ep in range(4):
+        even, odd = (dot(rows[s], table_ref[ep, s, 0]) + dot(rows[s], table_ref[ep, s, 1]) for s in range(2))
+        tiles = [slice(0, 128), slice(128, 256)]
+        near = [even[:, t] + odd[:, t] for t in tiles]
+        far = [even[:, t] - odd[:, t] for t in reversed(tiles)]
+        for e, z in ((ep, near), (ep + 4, far)):
+            n = 0
+            for p in range(pb):
+                out = [[None, None], [None, None]]
+                for kp in range(4):
+                    cs, sn = phase(p, e, kp)
+                    for t in range(2):
+                        q = [z[t][n + i * tgt : n + (i + 1) * tgt] for i in range(4)]
+                        re, im = q[0] * cs[t] + q[1] * sn[t], q[3] * cs[t] - q[2] * sn[t]
+                        out[0][t] = re if kp == 0 else out[0][t] + re
+                        out[1][t] = im if kp == 0 else out[1][t] + im
+                    n += 4 * tgt
+                store(p, e, out)
+
+
+def adjoint_level(y_ref, phase, table_ref, store, parents, tgt):
+    tb = min(tgt, 32)
+    pb, nt = min(parents, 32 // tb), tgt // tb
+
+    def body(i, carry):
+        p0, t0 = (i // nt) * pb, pl.multiple_of((i % nt) * tb, 8)
+
+        def load(p, k):
+            rows = pl.ds(pl.multiple_of(k * tgt + t0, 8), tb)
+            return [[y_ref[p0 + p, c, t, rows] for t in range(2)] for c in range(2)]
+
+        source = lambda p, e: (p0 + p) * 8 + e
+        adjoint_block(
+            load,
+            lambda p, e, kp: phase(source(p, e), kp),
+            table_ref,
+            lambda p, e, out: store(source(p, e), t0, tb, out),
+            pb, tb,
+        )
+        return carry
+
+    lax.fori_loop(0, (parents // pb) * nt, body, 0)
+
+
+def turn(x, c, s, sign=1):
+    if sign > 0:
+        return [[x[0][t] * c[t] - x[1][t] * s[t] for t in range(2)], [x[0][t] * s[t] + x[1][t] * c[t] for t in range(2)]]
+    return [[x[0][t] * c[t] + x[1][t] * s[t] for t in range(2)], [x[1][t] * c[t] - x[0][t] * s[t] for t in range(2)]]
+
+
+def pack(groups):
+    out, rest = [], []
+    for x in groups:
+        last = x[1][1]
+        for i, y in enumerate((x[0][0], x[0][1], x[1][0])):
+            out.append(jnp.concatenate([y[:, :HALF], last[:, 20 * i : 20 * i + 20]], axis=1))
+        rest.append(last[:, 60:HALF])
+    out.append(jnp.concatenate([rest[0], rest[0][:, :16], rest[1], rest[1][:, :16]], axis=1))
+    return out
+
+
+def unpack(x):
+    groups = []
+    for g in range(2):
+        y = x[3 * g : 3 * g + 3]
+        tail = x[6][:, 64 * g : 64 * g + 48]
+        last = jnp.concatenate([v[:, HALF:] for v in y] + [tail, tail[:, :20]], axis=1)
+        groups.append([[y[0], y[1]], [y[2], last]])
+    return groups
+
+
+def join_rows(groups):
+    return [[jnp.concatenate([g[c][t] for g in groups], axis=0) for t in range(2)] for c in range(2)]
+
+
+def grid_rows():
+    t, m = lane_points()
+    g = cheb_points(ORDER).astype(np.float32)
+    full = (np.repeat(g, ORDER * ORDER), np.tile(np.repeat(g, ORDER), ORDER), np.tile(g, ORDER**2))
+    out = np.zeros((8, 128), np.float32)
+    for d in range(3):
+        out[2 * d, :HALF], out[2 * d + 1, :HALF] = full[d][t], full[d][m]
+    return jnp.asarray(out)
+
+
+def bits_of(index, groups):
+    coords = [jnp.zeros_like(index) for _ in range(3)]
+    for group in range(groups):
+        digit = (index >> (3 * (groups - 1 - group))) & 7
+        coords = [c * 2 + ((digit >> b) & 1) for c, b in zip(coords, (2, 1, 0))]
+    return [c.astype(jnp.float32) for c in coords]
+
+
+def slopes_of(index, groups, t, grid_ref, med):
+    side = band / float(2**groups)
+    pts = [side * (c + grid_ref[2 * d + t : 2 * d + t + 1]) for d, c in enumerate(bits_of(index, groups))]
+    radius = jnp.sqrt(pts[0] * pts[0] + pts[1] * pts[1] + pts[2] * pts[2])
+    return [p + med[d + 1] * radius for d, p in enumerate(pts)], med[0] * radius
+
+
+def rows_index():
+    return lax.broadcasted_iota(jnp.int32, (8, 128), 0)
+
+
+def fill_level(w_ref, flat_ref, first, count, level, grid_ref, med, p0_ref=None):
+    def body(i, carry):
+        index = first + i * 8 + rows_index()
+        for t in range(2):
+            slopes, base = slopes_of(index, LEVELS - level, t, grid_ref, med)
+            if p0_ref is not None:
+                bc, bs = turn_of(base + 0.5 * (slopes[0] + slopes[1] + slopes[2]))
+            for kp in range(4):
+                u = 0.0
+                for bit, a in zip((kp // 4, kp // 2 % 2, kp % 2), slopes):
+                    u = u + ((bit - 0.5) / 2.0 ** (level + 2)) * a
+                c, s = turn_of(u)
+                flat_ref[t, pl.ds(i * 64 + kp, 8, stride=8)] = c
+                flat_ref[t, pl.ds(i * 64 + 4 + kp, 8, stride=8)] = s
+                if p0_ref is not None:
+                    c2, s2 = c * c - s * s, 2.0 * c * s
+                    cc, ss, cs, sc = bc * c2, bs * s2, bc * s2, bs * c2
+                    for k, v, w in ((kp, cc - ss, cs + sc), (7 - kp, cc + ss, sc - cs)):
+                        p0_ref[0, t, pl.ds(i * 64 + k, 8, stride=8)] = v
+                        p0_ref[1, t, pl.ds(i * 64 + k, 8, stride=8)] = w
+        for t in range(2):
+            for j in range(8):
+                w_ref[t, i * 8 + j] = flat_ref[t, pl.ds(pl.multiple_of(i * 64 + j * 8, 8), 8)]
+        return carry
+
+    lax.fori_loop(0, count // 8, body, 0)
+
+
+def take_tiles(read):
+    out = []
+    for n in (0, Q):
+        far = [read(n + a, n + a + 36) for a in (180, 144, 108)] + [read(n, n + 20)]
+        out.append([read(n, n + 128).T, jnp.concatenate(far, axis=0).T])
+    return out
+
+
+def put_tiles(x, write):
+    for c, n in ((0, 0), (1, Q)):
+        near, far = x[c][0].T, x[c][1].T
+        write(n, near[:HALF])
+        for i, a in enumerate((72, 36, 0)):
+            write(n + HALF + 36 * i, far[a : a + 36])
+
+
+def load_pairs(ref, *index):
+    return [[ref[(*index, c, t)] for t in range(2)] for c in range(2)]
+
+
+def load_rows(ref, rows):
+    return [[ref[c, t, rows] for t in range(2)] for c in range(2)]
+
+
+def whole_kernel(
+    geo, med, fw_ref, aw_hbm, grid_ref, ft_ref, at_hbm, fo_ref, ao_ref,
+    aw_ref, at_ref, xa, xb, xc, xd, xe, p0, w0, w1, w2, w3, flat, el, send_f, send_a, recv_f, recv_a,
+    send_sem, recv_sem, load_sem,
+):
+    D, m, T, nx, ny = geo
+    ix, iy = lax.axis_index("sx"), lax.axis_index("sy")
+    me_s, me_t = iy * nx + ix, ix * ny + iy
+    med = [med[i] for i in range(4)]
+    mesh_id = pl.DeviceIdType.MESH
+    at_target = lambda d: (d // ny, lax.rem(d, ny))
+    at_source = lambda d: (lax.rem(d, nx), d // nx)
+    barrier = pltpu.get_barrier_semaphore()
+
+    def greet(r, carry):
+        pl.semaphore_signal(barrier, inc=1, device_id=at_target(lax.rem(me_t + r, D)), device_id_type=mesh_id)
+        return carry
+
+    lax.fori_loop(1, D, greet, 0)
+    loads = [pltpu.make_async_copy(aw_hbm, aw_ref, load_sem.at[0]), pltpu.make_async_copy(at_hbm, at_ref, load_sem.at[1])]
+    for copy in loads:
+        copy.start()
+
+    mine = (me_t, me_s)
+    slot = (me_s, me_t)
+    send, recv = (send_f, send_a), (recv_f, recv_a)
+    place = (at_target, at_source)
+
+    def block_copy(w, p, d, q):
+        return pltpu.make_async_remote_copy(
+            src_ref=send[w].at[p, d], dst_ref=recv[w].at[p, q],
+            send_sem=send_sem.at[w, p, d], recv_sem=recv_sem.at[w, p, q],
+            device_id=place[w](d), device_id_type=mesh_id,
+        )
+
+    def over_others(first, step):
+        def body(r, carry):
+            step(lax.rem(first + r, D))
+            return carry
+
+        lax.fori_loop(1, D, body, 0)
+
+    def start_all(w, p):
+        over_others(mine[w], lambda d: block_copy(w, p, d, slot[w]).start())
+        for n in range(7):
+            recv[w][p, slot[w], n] = send[w][p, mine[w], n]
+
+    def wait_all(w, p):
+        over_others(slot[w], lambda q: block_copy(w, p, q, q).wait_recv())
+
+    def drain_all(w, p):
+        over_others(mine[w], lambda d: block_copy(w, p, d, slot[w]).wait_send())
+
+    src = me_s * (64 * m)
+    fill_level(w0, flat, src, 64 * m, 0, grid_ref, med, p0)
+    fill_level(w1, flat, src // 8, 8 * m, 1, grid_ref, med)
+
+    def bring(a, carry):
+        x = take_tiles(lambda i, j: fw_ref[a, i:j])
+        for c in range(2):
+            for t in range(2):
+                for i in range(8 * m):
+                    xa[c, t, pl.ds(i * 64 + a, 8, stride=8)] = x[c][t][i * 8 : i * 8 + 8]
+        return carry
+
+    lax.fori_loop(0, 8, bring, 0)
+    pl.semaphore_wait(barrier, D - 1)
+
+    def rows_of(ref, s):
+        return load_rows(ref, pl.ds(pl.multiple_of(s * 8, 8), 8))
+
+    def forward_half(p, carry):
+        def load(s):
+            cs, sn = rows_of(p0, p * 64 + s)
+            return turn(rows_of(xa, p * 64 + s), cs, sn)
+
+        forward_level(load, phase_of(w0, p * 64), ft_ref, xb, 8, 8)
+        forward_level(lambda s: load_pairs(xb, s), phase_of(w1, p * 8), ft_ref, xc, 1, 64)
+
+        def fill(i, carry):
+            for r in range(4):
+                d = i * 4 + r
+                groups = []
+                for g in range(T // 8):
+                    box = d * (T // 8) + g
+                    groups.append(load_rows(xc.at[0], pl.ds((box % 8) * 8 + box // 8, 8, stride=64)))
+                for n, v in enumerate(pack(groups)):
+                    send_f[p, d, n] = v
+            return carry
+
+        lax.fori_loop(0, D // 4, fill, 0)
+        start_all(0, p)
+        return carry
+
+    lax.fori_loop(0, m, forward_half, 0)
+
+    fill_level(w2, flat, 0, 64, 2, grid_ref, med)
+    fill_level(w3, flat, 0, 8, 3, grid_ref, med)
+    zero = jnp.zeros((8, 128), jnp.int32)
+
+    def low(k, carry):
+        for t in range(2):
+            v = 0.0
+            for c, a in zip(bits_of(k * 8 + rows_index(), 2), slopes_of(zero, 0, t, grid_ref, med)[0]):
+                v = v + ((c - 1.5) / 2.0 ** (LEVELS + 1)) * a
+            cs, sn = turn_of(v)
+            rows = pl.ds(pl.multiple_of(k * 8, 8), 8)
+            el[0, t, rows] = cs
+            el[1, t, rows] = sn
+        return carry
+
+    lax.fori_loop(0, 8, low, 0)
+
+    def high_phase(a):
+        out = ([], [])
+        for t in range(2):
+            slopes, u = slopes_of(zero, 0, t, grid_ref, med)
+            for c, s in zip(bits_of(zero + (me_t * T + a), LEVELS - 1), slopes):
+                u = u + ((c + 0.5) / 2.0 ** (LEVELS - 1)) * s
+            cs, sn = turn_of(u)
+            out[0].append(cs)
+            out[1].append(sn)
+        return out
+
+    for copy in loads:
+        copy.wait()
+
+    def take_targets(b, carry):
+        lanes = pl.ds(pl.multiple_of(b * 128, 128), 128)
+        x = take_tiles(lambda i, j: aw_ref[i:j, lanes])
+        for h in range(2):
+            a = b * 2 + h
+            hc, hs = high_phase(a)
+            for k in range(8):
+                rows = slice(h * 64 + k * 8, h * 64 + k * 8 + 8)
+                lc, ls = load_rows(el, slice(k * 8, k * 8 + 8))
+                y = turn(turn([[x[c][t][rows] for t in range(2)] for c in range(2)], lc, ls), hc, hs)
+                for c in range(2):
+                    for t in range(2):
+                        xd[0, c, t, pl.ds(k * T + a, 8, stride=8 * T)] = y[c][t]
+        return carry
+
+    lax.fori_loop(0, T // 2, take_targets, 0)
+
+    def keep_in(ref):
+        def store(s, t0, tb, out):
+            for c in range(2):
+                for t in range(2):
+                    ref[s, c, t, pl.ds(t0, tb)] = out[c][t]
+
+        return store
+
+    def fill_back(s, t0, tb, out):
+        groups = [[[out[c][t][g * 8 : g * 8 + 8] for t in range(2)] for c in range(2)] for g in range(T // 8)]
+        for n, v in enumerate(pack(groups)):
+            send_a[lax.rem(s, m), s // m, n] = v
+
+    adjoint_level(xd, phase_of(w3), at_ref, keep_in(xe), 1, 8 * T)
+    adjoint_level(xe, phase_of(w2), at_ref, fill_back, 8, T)
+    for p in range(m):
+        start_all(1, p)
+
+    for p in range(m):
+        wait_all(0, p)
+
+    def arrived(s):
+        return join_rows(unpack([recv_f[lax.rem(s, m), s // m, n] for n in range(7)]))
+
+    forward_level(arrived, phase_of(w2), ft_ref, xe, 8, T)
+    forward_level(lambda s: load_pairs(xe, s), phase_of(w3), ft_ref, xd, 1, 8 * T)
+
+    def put_targets(b, carry):
+        lanes = pl.ds(pl.multiple_of(b * 128, 128), 128)
+        parts = [[[], []], [[], []]]
+        for h in range(2):
+            a = b * 2 + h
+            hc, hs = high_phase(a)
+            for k in range(8):
+                lc, ls = load_rows(el, slice(k * 8, k * 8 + 8))
+                y = load_rows(xd.at[0], pl.ds(k * T + a, 8, stride=8 * T))
+                y = turn(turn(y, lc, ls, -1), hc, hs, -1)
+                for c in range(2):
+                    for t in range(2):
+                        parts[c][t].append(y[c][t])
+
+        def write(n, v):
+            fo_ref[n : n + v.shape[0], lanes] = v
+
+        put_tiles([[jnp.concatenate(parts[c][t], axis=0) for t in range(2)] for c in range(2)], write)
+        return carry
+
+    lax.fori_loop(0, T // 2, put_targets, 0)
+
+    def adjoint_half(p, carry):
+        wait_all(1, p)
+
+        def spread(i, carry):
+            for r in range(4):
+                d = i * 4 + r
+                for g, x in enumerate(unpack([recv_a[p, d, n] for n in range(7)])):
+                    box = d * (T // 8) + g
+                    for c in range(2):
+                        for t in range(2):
+                            xc[0, c, t, pl.ds((box % 8) * 8 + box // 8, 8, stride=64)] = x[c][t]
+            return carry
+
+        lax.fori_loop(0, D // 4, spread, 0)
+
+        def finish(s, t0, tb, out):
+            cs, sn = rows_of(p0, p * 64 + s)
+            out = turn(out, cs, sn, -1)
+            for c in range(2):
+                for t in range(2):
+                    xa[c, t, pl.ds(pl.multiple_of((p * 64 + s) * 8, 8), 8)] = out[c][t]
+
+        adjoint_level(xc, phase_of(w1, p * 8), at_ref, keep_in(xb), 1, 64)
+        adjoint_level(xb, phase_of(w0, p * 64), at_ref, finish, 8, 8)
+        return carry
+
+    lax.fori_loop(0, m, adjoint_half, 0)
+
+    def leave(a, carry):
+        x = [[jnp.concatenate([xa[c, t, pl.ds(i * 64 + a, 8, stride=8)] for i in range(8 * m)], axis=0) for t in range(2)] for c in range(2)]
+
+        def write(n, v):
+            ao_ref[a, n : n + v.shape[0]] = v
+
+        put_tiles(x, write)
+        return carry
+
+    lax.fori_loop(0, 8, leave, 0)
+    for w in range(2):
+        for p in range(m):
+            drain_all(w, p)
+
+
+def one_exchange_shards(forward_weights, adjoint_weights, medium):
+    nx, ny = lax.axis_size("sx"), lax.axis_size("sy")
+    D, S, R = nx * ny, forward_weights.shape[0], adjoint_weights.shape[0]
+    m, T = S // 64, R // 64
+    vmem, hbm = pl.BlockSpec(memory_space=pltpu.VMEM), pl.BlockSpec(memory_space=pl.ANY)
+    forward_table, adjoint_table = forward_parity_table(), adjoint_parity_table()
+    f32 = lambda *shape: pltpu.VMEM(shape, jnp.float32)
+    f, b = pl.pallas_call(
+        lambda *a: whole_kernel((D, m, T, nx, ny), *a),
+        in_specs=[pl.BlockSpec(memory_space=pltpu.SMEM), vmem, hbm, vmem, vmem, hbm],
+        out_specs=[vmem, vmem],
+        out_shape=[jax.ShapeDtypeStruct((2 * Q, R), jnp.float32), jax.ShapeDtypeStruct((8, 2 * Q, S), jnp.float32)],
+        scratch_shapes=[
+            f32(2 * Q, R), pltpu.VMEM(adjoint_table.shape, jnp.bfloat16),
+            f32(2, 2, S * 8, 128), f32(8, 2, 2, 64, 128), f32(1, 2, 2, 512, 128),
+            f32(1, 2, 2, 64 * T, 128), f32(8, 2, 2, 8 * T, 128), f32(2, 2, S * 8, 128),
+            f32(2, S, 8, 128), f32(2, S // 8, 8, 128), f32(2, 64, 8, 128), f32(2, 8, 8, 128),
+            f32(2, S * 8, 128), f32(2, 2, 64, 128),
+            *[f32(m, D, 7, 8, 128) for _ in range(4)],
+            pltpu.SemaphoreType.DMA((2, m, D)), pltpu.SemaphoreType.DMA((2, m, D)), pltpu.SemaphoreType.DMA((2,)),
+        ],
+        compiler_params=pltpu.CompilerParams(
+            vmem_limit_bytes=60 * 1024 * 1024, collective_id=0, has_side_effects=True
+        ),
+    )(medium, forward_weights.transpose(1, 2, 0), adjoint_weights.T, grid_rows(), forward_table, adjoint_table)
+    return f.T, b.transpose(0, 2, 1)
+
+
+def shards(forward_weights, adjoint_weights, medium):
+    devices = lax.axis_size("sx") * lax.axis_size("sy")
+    S, R = forward_weights.shape[0], adjoint_weights.shape[0]
+    one = S == 128 and 2 * devices == 64 and R == 1024 and forward_weights.shape[2] == 2 * Q
+    return (one_exchange_shards if one else general_shards)(forward_weights, adjoint_weights, medium)
+
+
 def solution(mesh):
     in_specs = (P(("sy", "sx"), None, None), P(("sx", "sy"), None), P())
     out_specs = (P(("sx", "sy"), None), P(None, ("sy", "sx"), None))

time: 276 us -> 114 us (0.41)
  local copies, waits for them, and re-layouts: 50.7 us -> 4.23 us
  other arithmetic: 41.6 us -> 0 us
  waiting for transfers between devices: 38.3 us -> 0 us
  starting transfers between devices: 19 us -> 0 us
  Pallas kernels: 123 us -> 108 us
    all_to_all x4 -> x0, waiting for transfers between devices: 38.3 us -> none  [the longest x2 19.5 us: shards(): x = lax.all_to_all(x, op, split_axis=0, concat_axis=0, tiled=True)]
    all_to_all x4 -> x0, starting transfers between devices: 19 us -> none  [the longest x2 9.67 us: shards(): x = lax.all_to_all(x, op, split_axis=0, concat_axis=0, tiled=True)]
    transpose x7 -> x0, local copies, waits for them, and re-layouts: 17.6 us -> none  [the longest x4 12.3 us: forward_level(): return out.swapaxes(2, 3).reshape(count // 8, 2, tgt * 8, q)]
    another operation x7 -> x0, local copies, waits for them, and re-layouts: 17 us -> none  [the longest x3 7.79 us: adjoint_level(): operand = y.reshape(count, 2, tgt // 8, 8, q).swapaxes(2, 3)]
    pallas_call x8 -> x1, Pallas kernels: 123 us -> 108 us  [one_exchange_shards(): pl.pallas_call(lambda *a: whole_kernel((D, m, T, nx, ny), *a), in_specs=[...]
    mul x6 -> x0, other arithmetic: 12.3 us -> none  [the longest x4 7.19 us: turn_of(): return (sign * c, sign * (s * y))]
    another operation x8 -> x0, other arithmetic: 9.31 us -> none  [the longest x4 4.51 us: child_phase(): return jnp.stack(turn_of(u), axis=1)]
    add x4 -> x0, other arithmetic: 8.44 us -> none  [the longest x3 6.59 us: point_slopes(): p + medium[d + 1] * radius]
  transfers between devices with their start and end apart: 4 -> 0, of which waited for: 2 -> 0; matrix products, arithmetic and copies ran while one was open for 19% -> 0% of each run, Pallas kernels for 22% -> 0%
where the time goes in v2:
time: 114 us; the launch traced here: 113 us
  Pallas kernels  108 us (95%)
  local copies, waits for them, and re-layouts  4.23 us (4%)
    pallas_call x1, Pallas kernels, one_exchange_shards(): pl.pallas_call(lambda *a: whole_kernel((D, m, T, nx, ny), *a), in_specs=[...  108 us
    unnamed x4, local copies, waits for them, and re-layouts  4.23 us

profile of v2, /device:TPU:0, one launch (start us, length us, event | category | flops | bytes accessed | tf_op | source)
XLA Modules:
  0.0 113.1 jit_solution(17099012947443024880)
XLA Ops:
  0.6 108.2 %shard_map.77 = (f32[432,1024]{1,0:T(8,128)}, f32[8,432,128]{2,1,0:T(8,128)}) custom-call(f32[4]{0:T(128)} %a_0_.1, f32[8,432,128]{2,1,0:T(8,128)} %bitcast.4, f32[432,1024]{1,0:T(8,128)} %bitcast.5, f32[8,128]{1,0:T(8,128)} %constant.8.clone.a_3_, bf16[4,2,256,256]{3,2,1,0:T(8,128)(2,1)} %constant.6.clone.a_4_, bf16[4,2,2,256,256]{4,3,2,1,0:T(8,128)(2,1)} %constant.7.clone.a_5_), custom_call_target="tpu_custom_call" | custom-call | tf_op jit(solution)/shard_map/pallas_call | solution.py:763
  108.9 0.0 copy-start
  108.9 3.0 %copy.10 = f32[1024,432]{0,1:T(8,128)} copy(f32[1024,432]{0,1:T(8,128)} %bitcast.7) | data formatting | bytes 3538944
  111.9 0.0 copy-done
  111.9 1.2 %copy.11 = f32[8,128,432]{1,2,0:T(8,128)} copy(f32[8,128,432]{1,2,0:T(8,128)S(1)} %bitcast.6) | data formatting | bytes 3538944
Async XLA Ops:
  108.9 3.0 %copy-start = (f32[8,432,128]{2,1,0:T(8,128)S(1)}, f32[8,432,128]{2,1,0:T(8,128)}, u32[]{:S(2)}) copy-start(f32[8,432,128]{2,1,0:T(8,128)} %get-tuple-element.5) | copy-start | bytes 5308420

commit v3 on v2

--- a/solution.py
+++ b/solution.py
@@ -278,7 +278,7 @@
 
 
 def adjoint_parity_table():
-    parts = [np.concatenate([x.swapaxes(-1, -2)] * 2, axis=2) for x in parity_tables()]
+    parts = [x.swapaxes(-1, -2) for x in parity_tables()]
     return jnp.asarray(np.stack(parts, axis=2))
 
 
@@ -465,8 +465,9 @@
     return lax.broadcasted_iota(jnp.int32, (8, 128), 0)
 
 
-def fill_level(w_ref, flat_ref, first, count, level, grid_ref, med, p0_ref=None):
-    def body(i, carry):
+def fill_level(w_ref, flat_ref, first, count, level, grid_ref, med, p0_ref=None, at=0):
+    def body(j, carry):
+        i = at + j
         index = first + i * 8 + rows_index()
         for t in range(2):
             slopes, base = slopes_of(index, LEVELS - level, t, grid_ref, med)
@@ -486,8 +487,8 @@
                         p0_ref[0, t, pl.ds(i * 64 + k, 8, stride=8)] = v
                         p0_ref[1, t, pl.ds(i * 64 + k, 8, stride=8)] = w
         for t in range(2):
-            for j in range(8):
-                w_ref[t, i * 8 + j] = flat_ref[t, pl.ds(pl.multiple_of(i * 64 + j * 8, 8), 8)]
+            for n in range(8):
+                w_ref[t, i * 8 + n] = flat_ref[t, pl.ds(pl.multiple_of(i * 64 + n * 8, 8), 8)]
         return carry
 
     lax.fori_loop(0, count // 8, body, 0)
@@ -518,8 +519,8 @@
 
 
 def whole_kernel(
-    geo, med, fw_ref, aw_hbm, grid_ref, ft_ref, at_hbm, fo_ref, ao_ref,
-    aw_ref, at_ref, xa, xb, xc, xd, xe, p0, w0, w1, w2, w3, flat, el, send_f, send_a, recv_f, recv_a,
+    geo, med, fw_hbm, aw_hbm, grid_ref, ft_hbm, at_hbm, fo_hbm, ao_hbm,
+    fw_ref, aw_ref, ft_ref, at_ref, fo_ref, ao_ref, xa, xb, xc, xd, xe, p0, w0, w1, w2, w3, flat, el, send_f, send_a, recv_f, recv_a,
     send_sem, recv_sem, load_sem,
 ):
     D, m, T, nx, ny = geo
@@ -536,8 +537,11 @@
         return carry
 
     lax.fori_loop(1, D, greet, 0)
-    loads = [pltpu.make_async_copy(aw_hbm, aw_ref, load_sem.at[0]), pltpu.make_async_copy(at_hbm, at_ref, load_sem.at[1])]
-    for copy in loads:
+    first_loads = [pltpu.make_async_copy(fw_hbm, fw_ref, load_sem.at[0]), pltpu.make_async_copy(ft_hbm, ft_ref, load_sem.at[1])]
+    loads = [pltpu.make_async_copy(aw_hbm, aw_ref, load_sem.at[2])]
+    for h in range(2):
+        loads.append(pltpu.make_async_copy(at_hbm, at_ref.at[:, :, :, pl.ds(128 * h, 128)], load_sem.at[3 + h]))
+    for copy in first_loads + loads:
         copy.start()
 
     mine = (me_t, me_s)
@@ -559,10 +563,13 @@
 
         lax.fori_loop(1, D, body, 0)
 
+    def keep_own(w, p):
+        for n in range(7):
+            recv[w][p, slot[w], n] = send[w][p, mine[w], n]
+
     def start_all(w, p):
         over_others(mine[w], lambda d: block_copy(w, p, d, slot[w]).start())
-        for n in range(7):
-            recv[w][p, slot[w], n] = send[w][p, mine[w], n]
+        keep_own(w, p)
 
     def wait_all(w, p):
         over_others(slot[w], lambda q: block_copy(w, p, q, q).wait_recv())
@@ -571,8 +578,14 @@
         over_others(mine[w], lambda d: block_copy(w, p, d, slot[w]).wait_send())
 
     src = me_s * (64 * m)
-    fill_level(w0, flat, src, 64 * m, 0, grid_ref, med, p0)
-    fill_level(w1, flat, src // 8, 8 * m, 1, grid_ref, med)
+
+    def fill_half(p):
+        fill_level(w0, flat, src, 64, 0, grid_ref, med, p0, p * 8)
+        fill_level(w1, flat, src // 8, 8, 1, grid_ref, med, None, p)
+
+    fill_half(0)
+    for copy in first_loads:
+        copy.wait()
 
     def bring(a, carry):
         x = take_tiles(lambda i, j: fw_ref[a, i:j])
@@ -588,27 +601,53 @@
     def rows_of(ref, s):
         return load_rows(ref, pl.ds(pl.multiple_of(s * 8, 8), 8))
 
+    per = T // 8
+    groups_of = 8 // per
+    span = groups_of // 2
+
     def forward_half(p, carry):
         def load(s):
             cs, sn = rows_of(p0, p * 64 + s)
             return turn(rows_of(xa, p * 64 + s), cs, sn)
 
+        @pl.when(p > 0)
+        def _():
+            fill_half(p)
+
         forward_level(load, phase_of(w0, p * 64), ft_ref, xb, 8, 8)
-        forward_level(lambda s: load_pairs(xb, s), phase_of(w1, p * 8), ft_ref, xc, 1, 64)
-
-        def fill(i, carry):
-            for r in range(4):
-                d = i * 4 + r
-                groups = []
-                for g in range(T // 8):
-                    box = d * (T // 8) + g
-                    groups.append(load_rows(xc.at[0], pl.ds((box % 8) * 8 + box // 8, 8, stride=64)))
-                for n, v in enumerate(pack(groups)):
-                    send_f[p, d, n] = v
+
+        def forward_part(r, carry):
+            rows = pl.ds(pl.multiple_of(r * 32, 32), 32)
+            forward_level(lambda s: load_rows(xb.at[s], rows), phase_of(w1, p * 8), ft_ref, xc, 1, 32)
+
+            def fill(a, carry):
+                for n in range(span):
+                    d = a * groups_of + r * span + n
+                    groups = []
+                    for g in range(per):
+                        groups.append(load_rows(xc.at[0], pl.ds((n * per + g) * 8 + a, 8, stride=32)))
+                    for i, v in enumerate(pack(groups)):
+                        send_f[p, d, i] = v
+                return carry
+
+            lax.fori_loop(0, 8, fill, 0)
+
+            def go(j, carry):
+                a = lax.rem(me_t // groups_of + j, 8)
+                for n in range(span):
+                    d = a * groups_of + r * span + n
+
+                    @pl.when(d != me_t)
+                    def _():
+                        block_copy(0, p, d, me_s).start()
+
+                return carry
+
+            lax.fori_loop(0, 8, go, 0)
             return carry
 
-        lax.fori_loop(0, D // 4, fill, 0)
-        start_all(0, p)
+        lax.fori_loop(0, 2, forward_part, 0)
+        keep_own(0, p)
         return carry
 
     lax.fori_loop(0, m, forward_half, 0)
@@ -709,6 +748,8 @@
         return carry
 
     lax.fori_loop(0, T // 2, put_targets, 0)
+    leaving = [pltpu.make_async_copy(fo_ref, fo_hbm, load_sem.at[0])]
+    leaving[0].start()
 
     def adjoint_half(p, carry):
         wait_all(1, p)
@@ -734,20 +775,32 @@
 
         adjoint_level(xc, phase_of(w1, p * 8), at_ref, keep_in(xb), 1, 64)
         adjoint_level(xb, phase_of(w0, p * 64), at_ref, finish, 8, 8)
-        return carry
+        for q in range(m):
+            pl.when(p == q)(lambda: leave(q))
+        return carry
+
+    def leave(p):
+        def body(a, carry):
+            x = [
+                [jnp.concatenate([xa[c, t, pl.ds((p * 8 + i) * 64 + a, 8, stride=8)] for i in range(8)], axis=0) for t in range(2)]
+                for c in range(2)
+            ]
+
+            def write(n, v):
+                ao_ref[a, n : n + v.shape[0], p * 64 : p * 64 + 64] = v
+
+            put_tiles(x, write)
+            if p == m - 1:
+                pltpu.make_async_copy(ao_ref.at[a], ao_hbm.at[a], load_sem.at[1 + a]).start()
+            return carry
+
+        lax.fori_loop(0, 8, body, 0)
 
     lax.fori_loop(0, m, adjoint_half, 0)
-
-    def leave(a, carry):
-        x = [[jnp.concatenate([xa[c, t, pl.ds(i * 64 + a, 8, stride=8)] for i in range(8 * m)], axis=0) for t in range(2)] for c in range(2)]
-
-        def write(n, v):
-            ao_ref[a, n : n + v.shape[0]] = v
-
-        put_tiles(x, write)
-        return carry
-
-    lax.fori_loop(0, 8, leave, 0)
+    for a in range(8):
+        leaving.append(pltpu.make_async_copy(ao_ref.at[a], ao_hbm.at[a], load_sem.at[1 + a]))
+    for copy in leaving:
+        copy.wait()
     for w in range(2):
         for p in range(m):
             drain_all(w, p)
@@ -762,17 +815,18 @@
     f32 = lambda *shape: pltpu.VMEM(shape, jnp.float32)
     f, b = pl.pallas_call(
         lambda *a: whole_kernel((D, m, T, nx, ny), *a),
-        in_specs=[pl.BlockSpec(memory_space=pltpu.SMEM), vmem, hbm, vmem, vmem, hbm],
-        out_specs=[vmem, vmem],
+        in_specs=[pl.BlockSpec(memory_space=pltpu.SMEM), hbm, hbm, vmem, hbm, hbm],
+        out_specs=[hbm, hbm],
         out_shape=[jax.ShapeDtypeStruct((2 * Q, R), jnp.float32), jax.ShapeDtypeStruct((8, 2 * Q, S), jnp.float32)],
         scratch_shapes=[
-            f32(2 * Q, R), pltpu.VMEM(adjoint_table.shape, jnp.bfloat16),
+            f32(8, 2 * Q, S), f32(2 * Q, R), pltpu.VMEM(forward_table.shape, jnp.bfloat16),
+            pltpu.VMEM((4, 2, 2, 256, 256), jnp.bfloat16), f32(2 * Q, R), f32(8, 2 * Q, S),
             f32(2, 2, S * 8, 128), f32(8, 2, 2, 64, 128), f32(1, 2, 2, 512, 128),
             f32(1, 2, 2, 64 * T, 128), f32(8, 2, 2, 8 * T, 128), f32(2, 2, S * 8, 128),
             f32(2, S, 8, 128), f32(2, S // 8, 8, 128), f32(2, 64, 8, 128), f32(2, 8, 8, 128),
             f32(2, S * 8, 128), f32(2, 2, 64, 128),
             *[f32(m, D, 7, 8, 128) for _ in range(4)],
-            pltpu.SemaphoreType.DMA((2, m, D)), pltpu.SemaphoreType.DMA((2, m, D)), pltpu.SemaphoreType.DMA((2,)),
+            pltpu.SemaphoreType.DMA((2, m, D)), pltpu.SemaphoreType.DMA((2, m, D)), pltpu.SemaphoreType.DMA((9,)),
         ],
         compiler_params=pltpu.CompilerParams(
             vmem_limit_bytes=60 * 1024 * 1024, collective_id=0, has_side_effects=True

time: 114 us -> 111 us (0.974)
  the two profiles are of different devices: /device:TPU:0 before, /device:TPU:9 now
where the time goes in v3:
time: 111 us; the launch traced here: 110 us
  Pallas kernels  106 us (95%)
  local copies, waits for them, and re-layouts  4.23 us (4%)
    pallas_call x1, Pallas kernels, one_exchange_shards(): pl.pallas_call(lambda *a: whole_kernel((D, m, T, nx, ny), *a), in_specs=[...  106 us
    unnamed x4, local copies, waits for them, and re-layouts  4.23 us

profile of v3, /device:TPU:9, one launch (start us, length us, event | category | flops | bytes accessed | tf_op | source)
XLA Modules:
  0.0 110.4 jit_solution(13758950669832668201)
XLA Ops:
  0.6 105.5 %shard_map.77 = (f32[432,1024]{1,0:T(8,128)}, f32[8,432,128]{2,1,0:T(8,128)}) custom-call(f32[4]{0:T(128)} %a_0_.1, f32[8,432,128]{2,1,0:T(8,128)} %bitcast.4, f32[432,1024]{1,0:T(8,128)} %bitcast.5, f32[8,128]{1,0:T(8,128)} %constant.8.clone.a_3_, bf16[4,2,256,256]{3,2,1,0:T(8,128)(2,1)} %constant.6.clone.a_4_, bf16[4,2,2,128,256]{4,3,2,1,0:T(8,128)(2,1)} %constant.7.clone.a_5_), custom_call_target="tpu_custom_call" | custom-call | tf_op jit(solution)/shard_map/pallas_call | solution.py:816
  106.1 0.0 copy-start
  106.2 3.0 %copy.10 = f32[1024,432]{0,1:T(8,128)} copy(f32[1024,432]{0,1:T(8,128)} %bitcast.7) | data formatting | bytes 3538944
  109.2 0.0 copy-done
  109.2 1.2 %copy.11 = f32[8,128,432]{1,2,0:T(8,128)} copy(f32[8,128,432]{1,2,0:T(8,128)S(1)} %bitcast.6) | data formatting | bytes 3538944
Async XLA Ops:
  106.1 3.0 %copy-start = (f32[8,432,128]{2,1,0:T(8,128)S(1)}, f32[8,432,128]{2,1,0:T(8,128)}, u32[]{:S(2)}) copy-start(f32[8,432,128]{2,1,0:T(8,128)} %get-tuple-element.5) | copy-start | bytes 5308420
